TPU v7x, 32 devices: a whole 2x2x4 slice. The times are simulated.
32 devices in a mesh: ctg: 8 (over y, x, core), br: 4 (over z).
Axes of the slice: x: 2, y: 2, z: 4, core: 2. Of those that a mesh axis runs over, the one named last changes fastest.
Arguments:
- base_vm: float32 [10240], P(('ctg', 'br')), may hold values from 0.95 to 1.05
- base_va: float32 [10240], P(('ctg', 'br')), may hold values from -0.6 to 0.6
- delta_state: float32 [64, 2, 10240], P('ctg', None, 'br'), may hold values from -0.18 to 0.18
- multipliers: float32 [64, 2, 10240], P('ctg', None, 'br'), may hold values from -6 to 6
- net_inj: float32 [64, 2, 10240], P('ctg', None, 'br'), may hold values from -6 to 6
- ang_grad: float32 [64, 10240], P('ctg', 'br'), may hold values from -6 to 6
- from_bus: int32 [13312], P('br'), may hold values from 0 to 10239
- to_bus: int32 [13312], P('br'), may hold values from 0 to 10239
- status: int32 [64, 13312], P('ctg', 'br'), may hold values 0 or 1
- conduct: float32 [13312], P('br'), may hold values from 1 to 5
- suscept: float32 [13312], P('br'), may hold values from -15 to -5
- charging: float32 [13312], P('br'), may hold values from 0.1 to 0.6
- rating: float32 [13312], P('br'), may hold values from 1 to 3
- slack: float32 [64, 13312], P('ctg', 'br'), may hold values from 0.05 to 2
- zdual: float32 [64, 13312], P('ctg', 'br'), may hold values from 0.05 to 2
Outputs:
- mismatch: float32 [64, 2, 10240], P('ctg', None, 'br')
- dual_res: float32 [64, 10240], P('ctg', 'br')
- limit_res: float32 [64, 13312], P('ctg', 'br')
- ctg_norms: float32 [64, 4], P('ctg')
- total_norms: float32 [4], replicated
All inputs are finite; a program needn't handle non-finite values. No bound on the sum of `status` on one device may be relied on, other than what follows from the above.
Results may differ from a plain program's by a relative error of at most 0.0003.
Values sent between devices are 32-bit elements; how exact they have to be, the bound alone decides.
A program may use at most 64 MiB of HBM per device.

v0:
```python
import math

import jax
import jax.numpy as jnp
from jax import lax
from jax.sharding import PartitionSpec as P


def block_size(span_total, other_side):
    limit = max(128, (1 << 23) // other_side)
    power = 1 << limit.bit_length() - 1
    return math.gcd(span_total, min(1024, power))


def select_cols(values, index_list):
    row_count, bus_count = values.shape
    col_count = index_list.shape[0]
    span_cols = block_size(bus_count, col_count)
    block_count = bus_count // span_cols
    tiles = values.reshape(row_count, block_count, span_cols).transpose(1, 0, 2)

    def add_block(running, item):
        segment, number = item
        labels = number * span_cols + lax.iota(jnp.int32, span_cols)
        onehot = (labels[:, None] == index_list[None, :]).astype(jnp.float32)
        running = running + jnp.dot(
            segment, onehot, precision=lax.Precision.HIGHEST, preferred_element_type=jnp.float32
        )
        return (running, None)

    start_zero = jnp.zeros((row_count, col_count), jnp.float32)
    numbers = jnp.arange(block_count, dtype=jnp.int32)
    result, _ = lax.scan(add_block, start_zero, (tiles, numbers))
    return result


def spread_rows(values, index_list, bus_count):
    row_count, col_count = values.shape
    span_cols = block_size(bus_count, col_count)
    block_count = bus_count // span_cols

    def one_block(carry, number):
        labels = number * span_cols + lax.iota(jnp.int32, span_cols)
        onehot = (index_list[:, None] == labels[None, :]).astype(jnp.float32)
        piece_sum = jnp.dot(
            values, onehot, precision=lax.Precision.HIGHEST, preferred_element_type=jnp.float32
        )
        return (carry, piece_sum)

    numbers = jnp.arange(block_count, dtype=jnp.int32)
    _, pieces = lax.scan(one_block, jnp.int32(0), numbers)
    return pieces.transpose(1, 0, 2).reshape(row_count, bus_count)


def branch_flows(
    volt_mag, volt_ang, mult_p, mult_q, from_idx, to_idx, conduct, suscept, charging, in_service
):
    scen_count = volt_mag.shape[0]
    stacked = jnp.concatenate([volt_mag, volt_ang, mult_p, mult_q], 0)
    at_from_end = select_cols(stacked, from_idx)
    at_to_end = select_cols(stacked, to_idx)
    volt_from = at_from_end[:scen_count]
    volt_to = at_to_end[:scen_count]
    angle_diff = at_from_end[scen_count : 2 * scen_count] - at_to_end[scen_count : 2 * scen_count]
    mp_from = at_from_end[2 * scen_count : 3 * scen_count]
    mq_from = at_from_end[3 * scen_count :]
    mp_to = at_to_end[2 * scen_count : 3 * scen_count]
    mq_to = at_to_end[3 * scen_count :]
    cos_diff = jnp.cos(angle_diff)
    sin_diff = jnp.sin(angle_diff)
    volt_prod = volt_from * volt_to
    p_from = conduct * volt_from * volt_from - volt_prod * (conduct * cos_diff + suscept * sin_diff)
    q_from = -(suscept + charging) * volt_from * volt_from - volt_prod * (
        conduct * sin_diff - suscept * cos_diff
    )
    p_to = conduct * volt_to * volt_to - volt_prod * (conduct * cos_diff - suscept * sin_diff)
    q_to = -(suscept + charging) * volt_to * volt_to + volt_prod * (
        conduct * sin_diff + suscept * cos_diff
    )
    flow_dual = volt_prod * (
        mp_from * (conduct * sin_diff - suscept * cos_diff)
        - mq_from * (conduct * cos_diff + suscept * sin_diff)
        + mp_to * (conduct * sin_diff + suscept * cos_diff)
        + mq_to * (conduct * cos_diff - suscept * sin_diff)
    )
    at_from = jnp.stack([p_from, q_from, flow_dual], 1) * in_service[:, None, :]
    at_to = jnp.stack([p_to, q_to, -flow_dual], 1) * in_service[:, None, :]
    return (at_from, at_to)


def sum_at_buses(from_vals, to_vals, from_idx, to_idx, offset, bus_count):
    scen_count = from_vals.shape[0]
    both_vals = jnp.concatenate([from_vals, to_vals], 2).reshape(scen_count * 3, -1)
    both_idx = jnp.concatenate([from_idx, to_idx], 0) - offset
    summed = spread_rows(both_vals, both_idx, bus_count)
    return summed.reshape(scen_count, 3, bus_count)


def per_device(
    base_vm,
    base_va,
    delta_state,
    multipliers,
    net_inj,
    ang_grad,
    from_bus,
    to_bus,
    status,
    conduct,
    suscept,
    charging,
    rating,
    slack,
    zdual,
):
    full_vm, full_va = (
        lax.all_gather(base_vm, ("ctg", "br"), axis=0, tiled=True),
        lax.all_gather(base_va, ("ctg", "br"), axis=0, tiled=True),
    )
    shifts, duals_all = (
        lax.all_gather(delta_state, "br", axis=2, tiled=True),
        lax.all_gather(multipliers, "br", axis=2, tiled=True),
    )
    volt_mag = full_vm[None, :] + shifts[:, 0]
    volt_ang = full_va[None, :] + shifts[:, 1]
    own_buses = delta_state.shape[2]
    offset = lax.axis_index("br") * own_buses
    in_service = status.astype(jnp.float32)
    at_from, at_to = branch_flows(
        volt_mag,
        volt_ang,
        duals_all[:, 0],
        duals_all[:, 1],
        from_bus,
        to_bus,
        conduct,
        suscept,
        charging,
        in_service,
    )
    limit_res = in_service * (
        at_from[:, 0] * at_from[:, 0] + at_from[:, 1] * at_from[:, 1] + slack - rating * rating
    )
    complement = in_service * (zdual * slack - 0.01)
    limit_part = jnp.sum(limit_res * limit_res, axis=1)
    comp_part = jnp.sum(complement * complement, axis=1)
    limit_sq, comp_sq = lax.psum((limit_part, comp_part), "br")
    every_from, every_to = (
        lax.all_gather(at_from, "br", axis=2, tiled=True),
        lax.all_gather(at_to, "br", axis=2, tiled=True),
    )
    ends_from, ends_to = (
        lax.all_gather(from_bus, "br", axis=0, tiled=True),
        lax.all_gather(to_bus, "br", axis=0, tiled=True),
    )
    summed = sum_at_buses(every_from, every_to, ends_from, ends_to, offset, own_buses)
    mismatch = summed[:, :2] - net_inj
    dual_res = summed[:, 2] + ang_grad
    mis_part = jnp.sum(mismatch * mismatch, axis=(1, 2))
    dual_part = jnp.sum(dual_res * dual_res, axis=1)
    mis_sq, dual_sq = lax.psum((mis_part, dual_part), "br")
    squares = jnp.stack([mis_sq, dual_sq, limit_sq, comp_sq], 1)
    ctg_norms = jnp.sqrt(squares)
    totals = lax.psum(jnp.sum(squares, axis=0), "ctg")
    total_norms = jnp.sqrt(totals / (delta_state.shape[0] * lax.axis_size("ctg")))
    return (mismatch, dual_res, limit_res, ctg_norms, total_norms)


def solution(mesh):
    placed = (
        P(("ctg", "br")),
        P(("ctg", "br")),
        P("ctg", None, "br"),
        P("ctg", None, "br"),
        P("ctg", None, "br"),
        P("ctg", "br"),
        P("br"),
        P("br"),
        P("ctg", "br"),
        P("br"),
        P("br"),
        P("br"),
        P("br"),
        P("ctg", "br"),
        P("ctg", "br"),
    )
    return jax.shard_map(
        per_device,
        mesh=mesh,
        in_specs=placed,
        out_specs=(P("ctg", None, "br"), P("ctg", "br"), P("ctg", "br"), P("ctg", None), P()),
        check_vma=False,
    )
```

profile of v0, /device:TPU:0, one launch (start us, length us, event | category | flops | bytes accessed | tf_op | source)
XLA Modules:
  0.0 480.9 jit_solution(18033969470416528919)
XLA Ops:
  10.7 19.8 %all_gather.27 = f32[8,2,10240]{2,0,1:T(8,128)S(1)} all-gather(f32[8,2,2560]{2,0,1:T(8,128)S(1)} %copy.26), channel_id=1, replica_groups=mesh['ctg'=8,'br'=4] {'br'}, dimensions={2}, use_global_device_ids=true | all-gather | bytes 819200 | tf_op jit(solution)/shard_map/all_gather | solution.py:121
  30.6 16.5 %all_gather.29 = f32[8,2,10240]{2,0,1:T(8,128)S(1)} all-gather(f32[8,2,2560]{2,0,1:T(8,128)S(1)} %copy.27), channel_id=1, replica_groups=mesh['ctg'=8,'br'=4] {'br'}, dimensions={2}, use_global_device_ids=true | all-gather | bytes 819200 | tf_op jit(solution)/shard_map/all_gather | solution.py:122
  47.3 92.3 %all-reduce.6.cloned.1.call-done = (f32[10240]{0:T(1024)}, f32[10240]{0:T(1024)}) async-done(((f32[10240]{0:T(1024)}, f32[10240]{0:T(1024)}), (f32[10240]{0:T(1024)}, f32[10240]{0:T(1024)})) %all-reduce.6.cloned.1.call-update) | async-done | bytes 81936
  141.4 57.5 %while.34 = (s32[]{:T(128)}, f32[32,3328]{1,0:T(8,128)S(1)}, f32[10,32,1024]{2,1,0:T(8,128)S(1)}, s32[10]{0:T(128)S(1)}, s32[3328]{0:T(1024)S(1)}, /*index=5*/s32[]{:T(128)}, s32[1]{0:T(128)}, s32[]{:T(128)}) while((s32[]{:T(128)}, f32[32,3328]{1,0:T(8,128)S(1)}, f32[10,32,1024]{2,1,0:T(8,128)S(1)}, s32[10]{0:T(128)S(1)}, ...), condition=%wide.region_3.4_spmd.clone, body=%wide.region_2.3_spmd.clone.sunk | while | flops 1312244736 | bytes 1007743 | solution.py:33
  142.7 4.5 fusion.70
  159.9 4.5 fusion.70
  165.7 4.5 fusion.70
  177.2 4.5 fusion.70
  182.9 4.5 fusion.70
  194.4 4.5 fusion.70
  199.0 57.5 %while.33 = (s32[]{:T(128)}, f32[32,3328]{1,0:T(8,128)S(1)}, f32[10,32,1024]{2,1,0:T(8,128)S(1)}, s32[10]{0:T(128)S(1)}, s32[3328]{0:T(1024)S(1)}, /*index=5*/s32[]{:T(128)}, s32[1]{0:T(128)}, s32[]{:T(128)}) while((s32[]{:T(128)}, f32[32,3328]{1,0:T(8,128)S(1)}, f32[10,32,1024]{2,1,0:T(8,128)S(1)}, s32[10]{0:T(128)S(1)}, ...), condition=%wide.region_1.2_spmd.clone, body=%wide.region_0.1_spmd.clone.sunk | while | flops 1312244736 | bytes 1007743 | solution.py:33
  206.0 4.5 fusion.67
  211.7 4.5 fusion.67
  223.2 4.5 fusion.67
  240.5 4.5 fusion.67
  246.2 4.5 fusion.67
  258.8 14.7 %all-gather = s32[4,1,3328]{2,1,0:T(1,128)S(1)} all-gather(s32[1,1,3328]{2,1,0:T(1,128)S(1)} %reshape.69), channel_id=1, replica_groups=mesh['ctg'=8,'br'=4] {'br'}, dimensions={0}, use_global_device_ids=true | all-gather | bytes 66560 | tf_op jit(solution)/shard_map/all_gather | solution.py:153
  273.5 14.6 %all-gather.1 = s32[4,1,3328]{2,1,0:T(1,128)S(1)} all-gather(s32[1,1,3328]{2,1,0:T(1,128)S(1)} %reshape.71), channel_id=1, replica_groups=mesh['ctg'=8,'br'=4] {'br'}, dimensions={0}, use_global_device_ids=true | all-gather | bytes 66560 | tf_op jit(solution)/shard_map/all_gather | solution.py:154
  293.2 32.5 %all-gather.7.cloned.1.call-done = f32[8,3,13312]{2,0,1:T(8,128)} async-done(((f32[8,3,3328]{2,0,1:T(8,128)}), f32[8,3,13312]{2,0,1:T(8,128)}) %all-gather.7.cloned.1.call-update) | async-done | bytes 1277968 | tf_op jit(solution)/shard_map/all_gather | solution.py:150
  332.1 116.5 %while.32 = (s32[]{:T(128)}, f32[10,24,256]{2,1,0:T(8,128)}, s32[26624]{0:T(1024)S(1)}, s32[10]{0:T(128)S(1)}, f32[24,26624]{1,0:T(8,128)}, /*index=5*/s32[]{:T(128)}, s32[1]{0:T(128)}) while((s32[]{:T(128)}, f32[10,24,256]{2,1,0:T(8,128)}, s32[26624]{0:T(1024)S(1)}, s32[10]{0:T(128)S(1)}, f32[24,26624]{1,0:T(8,128)}, /*index=5*/s32[]{:T(128)}, ...), condition=%wide.region_5.6_spmd, body=%wide.region_4.5_spmd.sunk | while | flops 1969750272 | bytes 2689641 | solution.py:51
  333.4 10.4 %fusion.64 = f32[10,24,256]{2,1,0:T(8,128)} fusion(f32[10,24,256]{2,1,0:T(8,128)} %get-tuple-element.341, s32[]{:T(128)} %get-tuple-element.340, f32[24,26624]{1,0:T(8,128)} %get-tuple-element.351, s32[256]{0:T(256)S(1)} %iota_add_fusion.6, s32[26624]{0:T(1024)S(1)} %get-tuple-element.349), kind=kOutput, calls=%fused_computation.5.clone.1 | convolution fusion | flops 1969750016 | bytes 2688512 | tf_op jit(solution)/shard_map/while/body/eval_jaxpr/dot_general | solution.py:45
  345.0 10.4 %fusion.64 = f32[10,24,256]{2,1,0:T(8,128)} fusion(f32[10,24,256]{2,1,0:T(8,128)} %get-tuple-element.341, s32[]{:T(128)} %get-tuple-element.340, f32[24,26624]{1,0:T(8,128)} %get-tuple-element.351, s32[256]{0:T(256)S(1)} %iota_add_fusion.6, s32[26624]{0:T(1024)S(1)} %get-tuple-element.349), kind=kOutput, calls=%fused_computation.5.clone.1 | convolution fusion | flops 1969750016 | bytes 2688512 | tf_op jit(solution)/shard_map/while/body/eval_jaxpr/dot_general | solution.py:45
  356.7 10.4 %fusion.64 = f32[10,24,256]{2,1,0:T(8,128)} fusion(f32[10,24,256]{2,1,0:T(8,128)} %get-tuple-element.341, s32[]{:T(128)} %get-tuple-element.340, f32[24,26624]{1,0:T(8,128)} %get-tuple-element.351, s32[256]{0:T(256)S(1)} %iota_add_fusion.6, s32[26624]{0:T(1024)S(1)} %get-tuple-element.349), kind=kOutput, calls=%fused_computation.5.clone.1 | convolution fusion | flops 1969750016 | bytes 2688512 | tf_op jit(solution)/shard_map/while/body/eval_jaxpr/dot_general | solution.py:45
  368.3 10.4 %fusion.64 = f32[10,24,256]{2,1,0:T(8,128)} fusion(f32[10,24,256]{2,1,0:T(8,128)} %get-tuple-element.341, s32[]{:T(128)} %get-tuple-element.340, f32[24,26624]{1,0:T(8,128)} %get-tuple-element.351, s32[256]{0:T(256)S(1)} %iota_add_fusion.6, s32[26624]{0:T(1024)S(1)} %get-tuple-element.349), kind=kOutput, calls=%fused_computation.5.clone.1 | convolution fusion | flops 1969750016 | bytes 2688512 | tf_op jit(solution)/shard_map/while/body/eval_jaxpr/dot_general | solution.py:45
  380.0 10.4 %fusion.64 = f32[10,24,256]{2,1,0:T(8,128)} fusion(f32[10,24,256]{2,1,0:T(8,128)} %get-tuple-element.341, s32[]{:T(128)} %get-tuple-element.340, f32[24,26624]{1,0:T(8,128)} %get-tuple-element.351, s32[256]{0:T(256)S(1)} %iota_add_fusion.6, s32[26624]{0:T(1024)S(1)} %get-tuple-element.349), kind=kOutput, calls=%fused_computation.5.clone.1 | convolution fusion | flops 1969750016 | bytes 2688512 | tf_op jit(solution)/shard_map/while/body/eval_jaxpr/dot_general | solution.py:45
  391.6 10.4 %fusion.64 = f32[10,24,256]{2,1,0:T(8,128)} fusion(f32[10,24,256]{2,1,0:T(8,128)} %get-tuple-element.341, s32[]{:T(128)} %get-tuple-element.340, f32[24,26624]{1,0:T(8,128)} %get-tuple-element.351, s32[256]{0:T(256)S(1)} %iota_add_fusion.6, s32[26624]{0:T(1024)S(1)} %get-tuple-element.349), kind=kOutput, calls=%fused_computation.5.clone.1 | convolution fusion | flops 1969750016 | bytes 2688512 | tf_op jit(solution)/shard_map/while/body/eval_jaxpr/dot_general | solution.py:45
  403.2 10.4 %fusion.64 = f32[10,24,256]{2,1,0:T(8,128)} fusion(f32[10,24,256]{2,1,0:T(8,128)} %get-tuple-element.341, s32[]{:T(128)} %get-tuple-element.340, f32[24,26624]{1,0:T(8,128)} %get-tuple-element.351, s32[256]{0:T(256)S(1)} %iota_add_fusion.6, s32[26624]{0:T(1024)S(1)} %get-tuple-element.349), kind=kOutput, calls=%fused_computation.5.clone.1 | convolution fusion | flops 1969750016 | bytes 2688512 | tf_op jit(solution)/shard_map/while/body/eval_jaxpr/dot_general | solution.py:45
  414.9 10.4 %fusion.64 = f32[10,24,256]{2,1,0:T(8,128)} fusion(f32[10,24,256]{2,1,0:T(8,128)} %get-tuple-element.341, s32[]{:T(128)} %get-tuple-element.340, f32[24,26624]{1,0:T(8,128)} %get-tuple-element.351, s32[256]{0:T(256)S(1)} %iota_add_fusion.6, s32[26624]{0:T(1024)S(1)} %get-tuple-element.349), kind=kOutput, calls=%fused_computation.5.clone.1 | convolution fusion | flops 1969750016 | bytes 2688512 | tf_op jit(solution)/shard_map/while/body/eval_jaxpr/dot_general | solution.py:45
  426.6 10.4 %fusion.64 = f32[10,24,256]{2,1,0:T(8,128)} fusion(f32[10,24,256]{2,1,0:T(8,128)} %get-tuple-element.341, s32[]{:T(128)} %get-tuple-element.340, f32[24,26624]{1,0:T(8,128)} %get-tuple-element.351, s32[256]{0:T(256)S(1)} %iota_add_fusion.6, s32[26624]{0:T(1024)S(1)} %get-tuple-element.349), kind=kOutput, calls=%fused_computation.5.clone.1 | convolution fusion | flops 1969750016 | bytes 2688512 | tf_op jit(solution)/shard_map/while/body/eval_jaxpr/dot_general | solution.py:45
  438.2 10.4 %fusion.64 = f32[10,24,256]{2,1,0:T(8,128)} fusion(f32[10,24,256]{2,1,0:T(8,128)} %get-tuple-element.341, s32[]{:T(128)} %get-tuple-element.340, f32[24,26624]{1,0:T(8,128)} %get-tuple-element.351, s32[256]{0:T(256)S(1)} %iota_add_fusion.6, s32[26624]{0:T(1024)S(1)} %get-tuple-element.349), kind=kOutput, calls=%fused_computation.5.clone.1 | convolution fusion | flops 1969750016 | bytes 2688512 | tf_op jit(solution)/shard_map/while/body/eval_jaxpr/dot_general | solution.py:45
  451.4 10.0 %all-reduce.3 = (f32[8,1]{0,1:T(1,128)S(1)}, f32[8,1]{0,1:T(1,128)S(1)}, f32[8,1]{0,1:T(1,128)S(1)}, f32[8,1]{0,1:T(1,128)S(1)}) all-reduce(f32[8,1]{0,1:T(1,128)S(1)} %bitcast.75, f32[8,1]{0,1:T(1,128)S(1)} %bitcast.74, f32[8,1]{0,1:T(1,128)S(1)} %bitcast.77, f32[8,1]{0,1:T(1,128)S(1)} %bitcast.76), channel_id=1, replica_groups=mesh['ctg'=8,'br'=4] {'br'}, use_global_device_ids=true, to_apply=%region_13.14 | all-reduce | flops 32 | bytes 256 | tf_op jit(solution)/shard_map/psum | solution.py:147
  462.1 11.8 %psum.39 = f32[4]{0:T(128)S(1)} all-reduce(f32[4]{0:T(128)S(1)} %get-tuple-element.188), channel_id=1, replica_groups=mesh['ctg'=8,'br'=4] {'ctg'}, use_global_device_ids=true, to_apply=%region_15.16 | all-reduce | flops 4 | bytes 32 | tf_op jit(solution)/shard_map/psum | solution.py:164
  (142 shorter events, 81.0 us)
Async XLA Ops:
  7.2 23.4 %copy-start.1 = (f32[8,2,2560]{2,1,0:T(2,128)S(1)}, f32[8,2,2560]{2,1,0:T(2,128)}, u32[]{:S(2)}) copy-start(f32[8,2,2560]{2,1,0:T(2,128)} %param.24) | copy-start | bytes 491524
  7.2 40.0 %copy-start.5 = (f32[3328]{0:T(1024)S(1)}, f32[3328]{0:T(1024)}, u32[]{:S(2)}) copy-start(f32[3328]{0:T(1024)} %param.31) | copy-start | bytes 39940
  7.2 40.0 %copy-start.11 = (f32[3328]{0:T(1024)S(1)}, f32[3328]{0:T(1024)}, u32[]{:S(2)}) copy-start(f32[3328]{0:T(1024)} %param.32) | copy-start | bytes 39940
  7.2 132.4 %all-reduce.6.cloned.1.call-start = ((), (), s32[]{:S(2)}) async-start(), calls=%async_computation.2 | async-start | bytes 163840
  7.3 40.0 %copy-start = (s32[8,3328]{1,0:T(8,128)S(1)}, s32[8,3328]{1,0:T(8,128)}, u32[]{:S(2)}) copy-start(s32[8,3328]{1,0:T(8,128)} %param.29) | copy-start | bytes 319492
  8.2 0.9 copy-start.4
  9.1 0.6 copy-start.3
  9.7 283.4 %all-gather.5.cloned.1.call-start = ((), (), s32[]{:S(2)}) async-start(), calls=%async_computation | async-start | bytes 1597440 | tf_op jit(solution)/shard_map/all_gather | solution.py:149
  47.2 94.2 %copy-start.13 = (s32[3328]{0:T(1024)S(1)}, s32[3328]{0:T(1024)}, u32[]{:S(2)}) copy-start(s32[3328]{0:T(1024)} %param.28) | copy-start | bytes 39940
  141.4 57.5 %copy-start.12 = (s32[3328]{0:T(1024)S(1)}, s32[3328]{0:T(1024)}, u32[]{:S(2)}) copy-start(s32[3328]{0:T(1024)} %param.27) | copy-start | bytes 39940
  198.9 57.5 %copy-start.9 = (f32[3328]{0:T(1024)S(1)}, f32[3328]{0:T(1024)}, u32[]{:S(2)}) copy-start(f32[3328]{0:T(1024)} %param.30) | copy-start | bytes 39940
  256.5 2.3 copy-start.10
  256.5 31.6 %copy-start.6 = (f32[8,3328]{1,0:T(8,128)S(1)}, f32[8,3328]{1,0:T(8,128)}, u32[]{:S(2)}) copy-start(f32[8,3328]{1,0:T(8,128)} %param.34) | copy-start | bytes 319492
  256.5 31.6 %copy-start.7 = (f32[8,3328]{1,0:T(8,128)S(1)}, f32[8,3328]{1,0:T(8,128)}, u32[]{:S(2)}) copy-start(f32[8,3328]{1,0:T(8,128)} %param.35) | copy-start | bytes 319492
  258.0 67.8 %all-gather.7.cloned.1.call-start = ((), (), s32[]{:S(2)}) async-start(), calls=%async_computation.1 | async-start | bytes 1597440 | tf_op jit(solution)/shard_map/all_gather | solution.py:150
  332.1 117.8 %copy-start.2 = (f32[8,2,2560]{2,1,0:T(2,128)S(1)}, f32[8,2,2560]{2,1,0:T(2,128)}, u32[]{:S(2)}) copy-start(f32[8,2,2560]{2,1,0:T(2,128)} %param.25) | copy-start | bytes 491524
  332.1 118.6 %copy-start.8 = (f32[8,2560]{1,0:T(8,128)S(1)}, f32[8,2560]{1,0:T(8,128)}, u32[]{:S(2)}) copy-start(f32[8,2560]{1,0:T(8,128)} %param.26) | copy-start | bytes 245764
Sparse Core Ops, SparseCore 0:
  14.2 125.3 all-reduce.5
  258.1 35.0 all-gather.4
  294.8 30.9 all-gather.6
where the time goes:
time: 482 us; the launch traced here: 481 us
  matrix products  193 us (40%)
  waiting for transfers between devices  129 us (27%)
  blocking collectives  87.4 us (18%)
  local copies, waits for them, and re-layouts  28.5 us (6%)
  loops' own time  20.3 us (4%)
  between operations  14.1 us (3%)
  other arithmetic  8.15 us (2%)
    dot_general x10, matrix products, one_block(): jnp.dot(values, onehot, precision=lax.Precision.HIGHEST, preferred_elemen...  104 us
    unnamed x4, waiting for transfers between devices  93.1 us
    dot_general x20, matrix products, add_block(): jnp.dot(segment, onehot, precision=lax.Precision.HIGHEST, preferred_eleme...  89.4 us
    all_gather x1, waiting for transfers between devices, per_device(): lax.all_gather(at_to, 'br', axis=2, tiled=True)  32.5 us
    all_gather x1, blocking collectives, per_device(): lax.all_gather(delta_state, 'br', axis=2, tiled=True)  19.8 us
    dynamic_slice x30, local copies, waits for them, and re-layouts, select_cols(): result, _ = lax.scan(add_block, start_zero, (tiles, numbers))  17.5 us
    all_gather x1, blocking collectives, per_device(): lax.all_gather(multipliers, 'br', axis=2, tiled=True)  16.5 us
    all_gather x1, blocking collectives, per_device(): lax.all_gather(from_bus, 'br', axis=0, tiled=True)  14.7 us
  transfers between devices with their start and end apart: 3, of which 3 were waited for; matrix products, arithmetic and copies ran while one was open for 1% of the time, Pallas kernels for 0%

commit v1 on v0

v1 whole, which is shorter than its diff:
```python
import functools

import jax
import jax.numpy as jnp
from jax import lax
from jax.experimental import pallas as pl
from jax.experimental.pallas import tpu as pltpu
from jax.sharding import PartitionSpec as P

LANES = 128
SPAN = 256
ROWS = 8
MESH = pl.DeviceIdType.MESH


def sin_cos(x):
    y = x * x
    sin_c = (1 / 6227020800, -1 / 39916800, 1 / 362880, -1 / 5040, 1 / 120, -1 / 6)
    cos_c = (-1 / 87178291200, 1 / 479001600, -1 / 3628800, 1 / 40320, -1 / 720, 1 / 24, -0.5)
    s = jnp.full_like(y, sin_c[0])
    for c in sin_c[1:]:
        s = s * y + c
    k = jnp.full_like(y, cos_c[0])
    for c in cos_c[1:]:
        k = k * y + c
    return x + x * y * s, 1.0 + y * k


def body(
    groups, ranks,
    base, delta, mult, net, ang, ends, params, rating, status3, status, slack, zdual,
    mis_out, dual_out, lim_out, norm_out, tot_out,
    dbuf, mbuf, ebuf, pbuf, stbuf, table, got, vals, left, onehot, acc,
    res, rbuf, flow, rflow, sqs, sqbuf,
    send, recv, sq_send, sq_recv,
):
    grp, me = lax.axis_index("ctg"), lax.axis_index("br")
    count = groups * ranks
    mine = grp * ranks + me
    per = dbuf.shape[1]
    nb, nl = delta.shape[2], ends.shape[1]
    scen = delta.shape[0]

    barrier = pltpu.get_barrier_semaphore()

    def greet(i, carry):
        peer = lax.rem(mine + i, count)
        pl.semaphore_signal(
            barrier, inc=1, device_id=(peer // ranks, lax.rem(peer, ranks)), device_id_type=MESH
        )
        return carry

    lax.fori_loop(1, count, greet, 0)
    pl.semaphore_wait(barrier, count - 1)

    def remote(src, dst, kind, step):
        return pltpu.make_async_remote_copy(
            src_ref=src, dst_ref=dst, send_sem=send.at[kind, step], recv_sem=recv.at[kind, step],
            device_id=(grp, lax.rem(me + step, ranks)), device_id_type=MESH,
        )

    first = []
    for step in range(1, ranks):
        peer = lax.rem(me + step, ranks)
        part = pl.ds(peer * per, per)
        first.append((
            remote(delta.at[part], dbuf.at[me], 0, step),
            remote(mult.at[part], mbuf.at[me], 1, step),
            remote(ends, ebuf.at[me], 2, step),
            remote(params, pbuf.at[me], 3, step),
            remote(status3.at[peer], stbuf.at[me], 4, step),
        ))
    for kind in range(5):
        for group in first:
            group[kind].start()

    own = pl.ds(me * per, per)
    dbuf[me] = delta[own]
    mbuf[me] = mult[own]
    ebuf[me] = ends[...]
    pbuf[me] = params[...]
    stbuf[me] = status3[me]
    table[...] = jnp.zeros_like(table)
    vals[...] = jnp.zeros_like(vals)
    acc[...] = jnp.zeros_like(acc)
    sqs[...] = jnp.zeros_like(sqs)
    live_own = status[...].astype(jnp.float32)
    comp = live_own * (zdual[...] * slack[...] - 0.01)
    sqs[:, 3:4] = jnp.sum(comp * comp, axis=1, keepdims=True)

    for group in first:
        for copy in group:
            copy.wait()

    for src in range(ranks):
        cols = slice(src * nb, (src + 1) * nb)
        for s in range(per):
            table[s : s + 1, cols] = base[0:1, cols] + dbuf[src, s, 0:1, :]
            table[per + s : per + s + 1, cols] = base[1:2, cols] + dbuf[src, s, 1:2, :]
            table[2 * per + s : 2 * per + s + 1, cols] = mbuf[src, s, 0:1, :]
            table[3 * per + s : 3 * per + s + 1, cols] = mbuf[src, s, 1:2, :]

    tiles = table.shape[1] // LANES
    high = table.shape[1] // SPAN

    def one_source(src, carry):
        def pick(t, c):
            cols = pl.ds(pl.multiple_of(t * LANES, LANES), LANES)
            for end in range(2):
                spot = jnp.broadcast_to(ebuf[src, end : end + 1, cols], (ROWS, LANES))
                low, tile = spot & (LANES - 1), spot >> 7
                found = jnp.zeros((ROWS, LANES), jnp.float32)
                for k in range(tiles):
                    piece = jnp.take_along_axis(
                        table[:, k * LANES : (k + 1) * LANES], low, axis=1, mode="promise_in_bounds"
                    )
                    found = jnp.where(tile == k, piece, found)
                got[end, :, cols] = found
            return c

        lax.fori_loop(0, nl // LANES, pick, 0)

        def quantity(end, q):
            return got[end, q * per : (q + 1) * per, :]

        vf, vt = quantity(0, 0), quantity(1, 0)
        sn, cs = sin_cos(quantity(0, 1) - quantity(1, 1))
        par = pbuf[src]
        g, b, h = par[0:1], par[1:2], par[2:3]
        live = stbuf[src].astype(jnp.float32)
        u = vf * vt
        gc_bs, gc_mbs = g * cs + b * sn, g * cs - b * sn
        gs_bc, gs_mbc = g * sn + b * cs, g * sn - b * cs
        bh = -(b + h)
        pf = live * (g * vf * vf - u * gc_bs)
        qf = live * (bh * vf * vf - u * gs_mbc)
        pt = live * (g * vt * vt - u * gc_mbs)
        qt = live * (bh * vt * vt + u * gs_bc)
        fd = live * u * (
            quantity(0, 2) * gs_mbc - quantity(0, 3) * gc_bs
            + quantity(1, 2) * gs_bc + quantity(1, 3) * gc_mbs
        )
        flow[src] = pf * pf + qf * qf
        vals[0, 0:per, :] = pf
        vals[0, per : 2 * per, :] = qf
        vals[0, 2 * per : 3 * per, :] = fd
        vals[1, 0:per, :] = pt
        vals[1, per : 2 * per, :] = qt
        vals[1, 2 * per : 3 * per, :] = -fd

        for end in range(2):
            def spread(t, c):
                cols = pl.ds(pl.multiple_of(t * LANES, LANES), LANES)
                spot = ebuf[src, end : end + 1, cols]
                low = jnp.broadcast_to(spot & (SPAN - 1), (SPAN, LANES))
                label = lax.broadcasted_iota(jnp.int32, (SPAN, LANES), 0)
                onehot[:, cols] = jnp.where(low == label, 1.0, 0.0).astype(jnp.bfloat16)
                row = jnp.broadcast_to(spot >> 8, (2 * ROWS, LANES))
                value = vals[end, :, cols]
                head = value.astype(jnp.bfloat16).astype(jnp.float32)
                both = jnp.concatenate([head, value - head], axis=0)
                for k in range(high):
                    left[k * 2 * ROWS : (k + 1) * 2 * ROWS, cols] = jnp.where(
                        row == k, both, 0.0
                    ).astype(jnp.bfloat16)
                return c

            lax.fori_loop(0, nl // LANES, spread, 0)
            acc[...] += lax.dot_general(
                left[...], onehot[...], (((1,), (1,)), ((), ())),
                preferred_element_type=jnp.float32,
            )
        return carry

    lax.fori_loop(0, ranks, one_source, 0)

    for k in range(high):
        at = k * SPAN
        row = k * 2 * ROWS
        res[at // nb, :, at % nb : at % nb + SPAN] = (
            acc[row : row + ROWS, :] + acc[row + ROWS : row + 2 * ROWS, :]
        )

    back = []
    for step in range(1, ranks):
        peer = lax.rem(me + step, ranks)
        back.append((
            remote(res.at[peer], rbuf.at[me], 5, step),
            remote(flow.at[peer], rflow.at[me], 6, step),
        ))
    for kind in range(2):
        for group in back:
            group[kind].start()
    rbuf[me] = res[me]
    rflow[me] = flow[me]
    for group in back:
        for copy in group:
            copy.wait()

    rate = rating[...] * rating[...]
    for src in range(ranks):
        sums = rbuf[src]
        for s in range(per):
            c = src * per + s
            total = jnp.zeros((1, 1), jnp.float32)
            for k in range(2):
                row = sums[k * per + s : k * per + s + 1, :] - net[c, k : k + 1, :]
                mis_out[c, k : k + 1, :] = row
                total = total + jnp.sum(row * row, axis=1, keepdims=True)
            sqs[c : c + 1, 0:1] = total
        rows = slice(src * per, (src + 1) * per)
        dual = sums[2 * per : 3 * per, :] + ang[rows, :]
        dual_out[rows, :] = dual
        sqs[rows, 1:2] = jnp.sum(dual * dual, axis=1, keepdims=True)
        lim = status[rows, :].astype(jnp.float32) * (rflow[src] + slack[rows, :] - rate)
        lim_out[rows, :] = lim
        sqs[rows, 2:3] = jnp.sum(lim * lim, axis=1, keepdims=True)

    sqbuf[mine] = sqs[...]

    def share(i):
        peer = lax.rem(mine + i, count)
        return pltpu.make_async_remote_copy(
            src_ref=sqbuf.at[mine], dst_ref=sqbuf.at[mine],
            send_sem=sq_send.at[i], recv_sem=sq_recv.at[i],
            device_id=(peer // ranks, lax.rem(peer, ranks)), device_id_type=MESH,
        )

    def begin(i, c):
        share(i).start()
        return c

    def finish(i, c):
        share(i).wait()
        return c

    lax.fori_loop(1, count, begin, 0)
    lax.fori_loop(1, count, finish, 0)

    def add(i, c):
        return c + sqbuf[i]

    zero = jnp.zeros((scen, LANES), jnp.float32)
    group_sum = zero
    for z in range(ranks):
        group_sum = group_sum + sqbuf[grp * ranks + z]
    norm_out[...] = jnp.sqrt(group_sum[:, 0:4])
    everything = jnp.sum(lax.fori_loop(0, count, add, zero), axis=0, keepdims=True)
    tot_out[...] = jnp.sqrt(everything[:, 0:4] / (scen * groups))


def per_device(
    base_vm, base_va, delta_state, multipliers, net_inj, ang_grad, from_bus, to_bus,
    status, conduct, suscept, charging, rating, slack, zdual,
):
    groups, ranks = lax.axis_size("ctg"), lax.axis_size("br")
    count = groups * ranks
    scen, _, nb = delta_state.shape
    nl = from_bus.shape[0]
    per = scen // ranks
    buses = nb * ranks
    high = buses // SPAN
    base = lax.all_gather(jnp.stack([base_vm, base_va]), ("ctg", "br"), axis=1, tiled=True)
    ends = jnp.stack([from_bus, to_bus])
    params = jnp.stack([conduct, suscept, charging])
    f32 = jnp.float32
    vmem = pl.BlockSpec(memory_space=pltpu.VMEM)
    mis, dual, lim, norms, tot = pl.pallas_call(
        functools.partial(body, groups, ranks),
        out_shape=(
            jax.ShapeDtypeStruct((scen, 2, nb), f32),
            jax.ShapeDtypeStruct((scen, nb), f32),
            jax.ShapeDtypeStruct((scen, nl), f32),
            jax.ShapeDtypeStruct((scen, 4), f32),
            jax.ShapeDtypeStruct((1, 4), f32),
        ),
        in_specs=[vmem] * 12,
        out_specs=(vmem,) * 5,
        scratch_shapes=[
            pltpu.VMEM((ranks, per, 2, nb), f32),
            pltpu.VMEM((ranks, per, 2, nb), f32),
            pltpu.VMEM((ranks, 2, nl), jnp.int32),
            pltpu.VMEM((ranks, 3, nl), f32),
            pltpu.VMEM((ranks, per, nl), jnp.int32),
            pltpu.VMEM((ROWS, buses), f32),
            pltpu.VMEM((2, ROWS, nl), f32),
            pltpu.VMEM((2, ROWS, nl), f32),
            pltpu.VMEM((high * 2 * ROWS, nl), jnp.bfloat16),
            pltpu.VMEM((SPAN, nl), jnp.bfloat16),
            pltpu.VMEM((high * 2 * ROWS, SPAN), f32),
            pltpu.VMEM((ranks, ROWS, nb), f32),
            pltpu.VMEM((ranks, ROWS, nb), f32),
            pltpu.VMEM((ranks, per, nl), f32),
            pltpu.VMEM((ranks, per, nl), f32),
            pltpu.VMEM((scen, LANES), f32),
            pltpu.VMEM((count, scen, LANES), f32),
            pltpu.SemaphoreType.DMA((7, ranks)),
            pltpu.SemaphoreType.DMA((7, ranks)),
            pltpu.SemaphoreType.DMA((count,)),
            pltpu.SemaphoreType.DMA((count,)),
        ],
        compiler_params=pltpu.CompilerParams(
            collective_id=0, has_side_effects=True, vmem_limit_bytes=48 << 20
        ),
    )(
        base, delta_state, multipliers, net_inj, ang_grad, ends, params, rating[None, :],
        status.reshape(ranks, per, nl), status, slack, zdual,
    )
    return (mis, dual, lim, norms, tot[0])


def solution(mesh):
    placed = (
        P(("ctg", "br")), P(("ctg", "br")),
        P("ctg", None, "br"), P("ctg", None, "br"), P("ctg", None, "br"), P("ctg", "br"),
        P("br"), P("br"), P("ctg", "br"), P("br"), P("br"), P("br"), P("br"),
        P("ctg", "br"), P("ctg", "br"),
    )
    return jax.shard_map(
        per_device,
        mesh=mesh,
        in_specs=placed,
        out_specs=(P("ctg", None, "br"), P("ctg", "br"), P("ctg", "br"), P("ctg", None), P()),
        check_vma=False,
    )
```

time: 482 us -> 175 us (0.36)
  matrix products: 193 us -> 0 us
  waiting for transfers between devices: 129 us -> 0 us
  Pallas kernels: 0 us -> 96.5 us
  local copies, waits for them, and re-layouts: 28.5 us -> 6.27 us
  loops' own time: 20.3 us -> 0 us
  blocking collectives: 87.4 us -> 70.6 us
  between operations: 14.1 us -> 0.88 us
  other arithmetic: 8.15 us -> 0.08 us
    dot_general x30 -> x0, matrix products: 193 us -> none  [the longest x10 104 us: one_block(): jnp.dot(values, onehot, precision=lax.Precision.HIGHEST, preferred_elemen...]
    pallas_call x0 -> x1, Pallas kernels: none -> 96.5 us  [per_device(): pl.pallas_call(functools.partial(body, groups, ranks), out_shape=(jax.Sha...]
    unnamed x4 -> x0, waiting for transfers between devices: 93.1 us -> none
    all_gather x2 -> x0, waiting for transfers between devices: 35.8 us -> none  [the longest x1 32.5 us: per_device(): lax.all_gather(at_to, 'br', axis=2, tiled=True)]
    psum x2 -> x0, blocking collectives: 21.7 us -> none  [the longest x1 11.8 us: per_device(): totals = lax.psum(jnp.sum(squares, axis=0), 'ctg')]
    another operation x3 -> x0, loops' own time: 20.3 us -> none  [the longest x2 13.7 us: select_cols(): result, _ = lax.scan(add_block, start_zero, (tiles, numbers))]
    dynamic_slice x30 -> x0, local copies, waits for them, and re-layouts: 17.5 us -> none  [select_cols(): result, _ = lax.scan(add_block, start_zero, (tiles, numbers))]
    all_gather x4 -> x1, blocking collectives: 65.6 us -> 70.6 us  [per_device(): lax.all_gather(jnp.stack([base_vm, base_va]), ('ctg', 'br'), axis=1, tile...]
  transfers between devices with their start and end apart: 3 -> 0, of which waited for: 3 -> 0; matrix products, arithmetic and copies ran while one was open for 1% -> 0% of each run, Pallas kernels for 0% -> 0%
where the time goes in v1:
time: 175 us; the launch traced here: 174 us
  Pallas kernels  96.5 us (55%)
  blocking collectives  70.6 us (40%)
  local copies, waits for them, and re-layouts  6.27 us (4%)
    pallas_call x1, Pallas kernels, per_device(): pl.pallas_call(functools.partial(body, groups, ranks), out_shape=(jax.Sha...  96.5 us
    all_gather x1, blocking collectives, per_device(): lax.all_gather(jnp.stack([base_vm, base_va]), ('ctg', 'br'), axis=1, tile...  70.6 us
    unnamed x32, local copies, waits for them, and re-layouts  4.72 us

profile of v1, /device:TPU:0, one launch (start us, length us, event | category | flops | bytes accessed | tf_op | source)
XLA Modules:
  0.0 174.4 jit_solution(1432081842119325100)
XLA Ops:
  0.6 0.0 copy-start.12
  0.6 0.7 stack.30
  1.3 0.0 copy-done.12
  1.3 0.0 copy-start.7
  1.4 0.0 copy-start.10
  1.4 0.7 stack.33
  2.1 0.0 copy-done.7
  2.1 0.0 copy-start.8
  2.1 0.0 copy-start.9
  2.2 0.0 copy-start.6
  2.2 0.6 copy-done.8
  2.9 0.0 copy-done.9
  2.9 0.0 copy-start.5
  2.9 0.0 copy-done.10
  2.9 0.0 copy-start.4
  3.0 0.0 copy-done.11
  3.0 0.0 copy-start.3
  3.0 70.6 %all-gather = f32[32,320,2]{1,2,0:T(2,128)S(1)} all-gather(f32[1,320,2]{1,2,0:T(2,128)S(1)} %maximum_bitcast_fusion), channel_id=1, replica_groups=mesh['ctg'=8,'br'=4] {'ctg','br'}, dimensions={0}, use_global_device_ids=true | all-gather | bytes 84480 | tf_op jit(solution)/shard_map/all_gather | solution.py:263
  73.6 0.0 copy-start
  73.6 0.0 copy-start.1
  73.7 0.1 reshape.15
  73.8 0.8 copy-done
  74.6 0.1 reshape.13.status3
  74.6 0.0 copy-done.6
  74.6 0.0 copy-done.5
  74.7 0.0 copy-done.4
  74.7 96.5 %shard_map.182 = (f32[8,2,2560]{2,1,0:T(2,128)S(1)}, f32[8,2560]{1,0:T(8,128)S(1)}, f32[8,3328]{1,0:T(8,128)S(1)}, f32[8,4]{1,0:T(8,128)S(1)}, f32[1,4]{1,0:T(1,128)S(1)}) custom-call(f32[2,10240]{1,0:T(2,128)S(1)} %bitcast.8, f32[8,2,2560]{2,1,0:T(2,128)S(1)} %copy-done.1, f32[8,2,2560]{2,1,0:T(2,128)S(1)} %copy-done.2, f32[8,2,2560]{2,1,0:T(2,128)S(1)} %copy-done.3, ...), custom_call_target="tpu_custom_call" | custom-call | tf_op jit(solution)/shard_map/pallas_call | solution.py:268
  171.2 0.7 copy.22
  171.9 0.7 copy.27
  172.6 0.6 copy.28
  173.2 0.6 copy.29
  173.8 0.5 copy.30
  (15 shorter events, 0.1 us)
Async XLA Ops:
  0.6 0.7 copy-start.12
  1.3 1.7 copy-start.11
  1.3 0.8 copy-start.7
  1.4 1.5 copy-start.10
  2.1 0.7 copy-start.8
  2.1 0.7 copy-start.9
  2.2 72.5 %copy-start.6 = (f32[8,2560]{1,0:T(8,128)S(1)}, f32[8,2560]{1,0:T(8,128)}, u32[]{:S(2)}) copy-start(f32[8,2560]{1,0:T(8,128)} %ang.1) | copy-start | bytes 245764
  2.9 71.8 %copy-start.5 = (f32[8,3328]{1,0:T(8,128)S(1)}, f32[8,3328]{1,0:T(8,128)}, u32[]{:S(2)}) copy-start(f32[8,3328]{1,0:T(8,128)} %zdual.1) | copy-start | bytes 319492
  2.9 71.7 %copy-start.4 = (f32[8,3328]{1,0:T(8,128)S(1)}, f32[8,3328]{1,0:T(8,128)}, u32[]{:S(2)}) copy-start(f32[8,3328]{1,0:T(8,128)} %slack.1) | copy-start | bytes 319492
  3.0 71.6 %copy-start.3 = (f32[8,2,2560]{2,1,0:T(2,128)S(1)}, f32[8,2,2560]{2,1,0:T(2,128)}, u32[]{:S(2)}) copy-start(f32[8,2,2560]{2,1,0:T(2,128)} %net.1) | copy-start | bytes 491524
  73.6 1.1 copy-start.2
  73.6 0.9 copy-start
  73.6 1.0 copy-start.1

commit v2 on v1

--- a/solution.py
+++ b/solution.py
@@ -30,9 +30,9 @@
     groups, ranks,
     base, delta, mult, net, ang, ends, params, rating, status3, status, slack, zdual,
     mis_out, dual_out, lim_out, norm_out, tot_out,
-    dbuf, mbuf, ebuf, pbuf, stbuf, table, got, vals, left, onehot, acc,
+    bbuf, dbuf, mbuf, ebuf, pbuf, stbuf, table, got, vals, left, onehot, acc,
     res, rbuf, flow, rflow, sqs, sqbuf,
-    send, recv, sq_send, sq_recv,
+    send, recv, base_send, base_recv, sq_send, sq_recv,
 ):
     grp, me = lax.axis_index("ctg"), lax.axis_index("br")
     count = groups * ranks
@@ -59,6 +59,22 @@
             device_id=(grp, lax.rem(me + step, ranks)), device_id_type=MESH,
         )
 
+    def all_peers(slots, block, sends, recvs, i):
+        peer = lax.rem(mine + i, count)
+        return pltpu.make_async_remote_copy(
+            src_ref=block, dst_ref=slots.at[mine], send_sem=sends.at[i], recv_sem=recvs.at[i],
+            device_id=(peer // ranks, lax.rem(peer, ranks)), device_id_type=MESH,
+        )
+
+    def begin_base(i, c):
+        all_peers(bbuf, base, base_send, base_recv, i).start()
+        return c
+
+    def finish_base(i, c):
+        all_peers(bbuf, base, base_send, base_recv, i).wait()
+        return c
+
+    lax.fori_loop(1, count, begin_base, 0)
     first = []
     for step in range(1, ranks):
         peer = lax.rem(me + step, ranks)
@@ -75,6 +91,7 @@
             group[kind].start()
 
     own = pl.ds(me * per, per)
+    bbuf[mine] = base[...]
     dbuf[me] = delta[own]
     mbuf[me] = mult[own]
     ebuf[me] = ends[...]
@@ -88,15 +105,17 @@
     comp = live_own * (zdual[...] * slack[...] - 0.01)
     sqs[:, 3:4] = jnp.sum(comp * comp, axis=1, keepdims=True)
 
+    lax.fori_loop(1, count, finish_base, 0)
     for group in first:
         for copy in group:
             copy.wait()
 
     for src in range(ranks):
         cols = slice(src * nb, (src + 1) * nb)
+        volts = jnp.concatenate([bbuf[src * groups + i] for i in range(groups)], axis=1)
         for s in range(per):
-            table[s : s + 1, cols] = base[0:1, cols] + dbuf[src, s, 0:1, :]
-            table[per + s : per + s + 1, cols] = base[1:2, cols] + dbuf[src, s, 1:2, :]
+            table[s : s + 1, cols] = volts[0:1] + dbuf[src, s, 0:1, :]
+            table[per + s : per + s + 1, cols] = volts[1:2] + dbuf[src, s, 1:2, :]
             table[2 * per + s : 2 * per + s + 1, cols] = mbuf[src, s, 0:1, :]
             table[3 * per + s : 3 * per + s + 1, cols] = mbuf[src, s, 1:2, :]
 
@@ -218,20 +237,12 @@
 
     sqbuf[mine] = sqs[...]
 
-    def share(i):
-        peer = lax.rem(mine + i, count)
-        return pltpu.make_async_remote_copy(
-            src_ref=sqbuf.at[mine], dst_ref=sqbuf.at[mine],
-            send_sem=sq_send.at[i], recv_sem=sq_recv.at[i],
-            device_id=(peer // ranks, lax.rem(peer, ranks)), device_id_type=MESH,
-        )
-
     def begin(i, c):
-        share(i).start()
+        all_peers(sqbuf, sqbuf.at[mine], sq_send, sq_recv, i).start()
         return c
 
     def finish(i, c):
-        share(i).wait()
+        all_peers(sqbuf, sqbuf.at[mine], sq_send, sq_recv, i).wait()
         return c
 
     lax.fori_loop(1, count, begin, 0)
@@ -260,7 +271,7 @@
     per = scen // ranks
     buses = nb * ranks
     high = buses // SPAN
-    base = lax.all_gather(jnp.stack([base_vm, base_va]), ("ctg", "br"), axis=1, tiled=True)
+    base = jnp.stack([base_vm, base_va])
     ends = jnp.stack([from_bus, to_bus])
     params = jnp.stack([conduct, suscept, charging])
     f32 = jnp.float32
@@ -277,6 +288,7 @@
         in_specs=[vmem] * 12,
         out_specs=(vmem,) * 5,
         scratch_shapes=[
+            pltpu.VMEM((count, 2, base_vm.shape[0]), f32),
             pltpu.VMEM((ranks, per, 2, nb), f32),
             pltpu.VMEM((ranks, per, 2, nb), f32),
             pltpu.VMEM((ranks, 2, nl), jnp.int32),
@@ -298,6 +310,8 @@
             pltpu.SemaphoreType.DMA((7, ranks)),
             pltpu.SemaphoreType.DMA((count,)),
             pltpu.SemaphoreType.DMA((count,)),
+            pltpu.SemaphoreType.DMA((count,)),
+            pltpu.SemaphoreType.DMA((count,)),
         ],
         compiler_params=pltpu.CompilerParams(
             collective_id=0, has_side_effects=True, vmem_limit_bytes=48 << 20

time: 175 us -> 113 us (0.65)
  blocking collectives: 70.6 us -> 0 us
  Pallas kernels: 96.5 us -> 102 us
  local copies, waits for them, and re-layouts: 6.27 us -> 9.08 us
    all_gather x1 -> x0, blocking collectives: 70.6 us -> none  [per_device(): lax.all_gather(jnp.stack([base_vm, base_va]), ('ctg', 'br'), axis=1, tile...]
    pallas_call x1, Pallas kernels: 96.5 us -> 102 us  [per_device(): pl.pallas_call(functools.partial(body, groups, ranks), out_shape=(jax.Sha...]
    unnamed x32 -> x29, local copies, waits for them, and re-layouts: 4.72 us -> 6.77 us
where the time goes in v2:
time: 113 us; the launch traced here: 112 us
  Pallas kernels  102 us (90%)
  local copies, waits for them, and re-layouts  9.08 us (8%)
    pallas_call x1, Pallas kernels, per_device(): pl.pallas_call(functools.partial(body, groups, ranks), out_shape=(jax.Sha...  102 us
    unnamed x29, local copies, waits for them, and re-layouts  6.77 us

profile of v2, /device:TPU:0, one launch (start us, length us, event | category | flops | bytes accessed | tf_op | source)
XLA Modules:
  0.0 112.3 jit_solution(11557212791465936919)
XLA Ops:
  0.6 0.0 copy-start.11
  0.6 0.0 copy-start.10
  0.7 0.7 stack.30
  1.3 0.0 copy-done.11
  1.4 0.0 copy-start.7
  1.4 0.0 copy-start.8
  1.4 0.0 copy-start.9
  1.4 0.7 stack.33
  2.1 0.0 copy-done.7
  2.1 0.0 copy-start.2
  2.2 0.0 copy-done.8
  2.2 0.0 copy-start
  2.3 0.0 copy-done.9
  2.3 0.0 copy-done.10
  2.3 0.0 copy-start.1
  2.4 0.8 broadcast_in_dim.3.rating
  3.1 0.0 copy-done
  3.2 0.1 reshape.13.status3
  3.2 0.0 copy-done.2
  3.2 0.0 copy-done.1
  3.3 0.0 copy-start.3
  3.3 0.9 copy-done.3
  4.2 0.0 copy-start.4
  4.2 0.9 copy-done.4
  5.1 0.9 copy-done.5
  6.0 0.9 copy-done.6
  6.8 102.4 %shard_map.182 = (f32[8,2,2560]{2,1,0:T(2,128)S(1)}, f32[8,2560]{1,0:T(8,128)S(1)}, f32[8,3328]{1,0:T(8,128)S(1)}, f32[8,4]{1,0:T(8,128)S(1)}, f32[1,4]{1,0:T(1,128)S(1)}) custom-call(f32[2,320]{1,0:T(2,128)S(1)} %pad_maximum_fusion.1.base, f32[8,2,2560]{2,1,0:T(2,128)S(1)} %copy-done.1, f32[8,2,2560]{2,1,0:T(2,128)S(1)} %copy-done.2, ...), custom_call_target="tpu_custom_call" | custom-call | tf_op jit(solution)/shard_map/pallas_call | solution.py:279
  109.2 0.7 copy.20
  109.9 0.7 copy.25
  110.5 0.6 copy.26
  111.2 0.6 copy.27
  111.8 0.5 copy.28
  (10 shorter events, 0.1 us)
Async XLA Ops:
  0.6 0.7 copy-start.11
  0.6 1.6 %copy-start.10 = (f32[3328]{0:T(1024)S(1)}, f32[3328]{0:T(1024)}, u32[]{:S(2)}) copy-start(f32[3328]{0:T(1024)} %param.26) | copy-start | bytes 39940
  1.4 0.8 copy-start.7
  1.4 0.8 copy-start.8
  1.4 0.9 copy-start.9
  2.1 1.1 copy-start.2
  2.2 0.9 copy-start
  2.3 0.9 copy-start.1
  3.3 0.9 copy-start.3
  4.2 0.9 copy-start.4
  5.1 0.9 copy-start.5
  6.0 0.9 copy-start.6

commit v3 on v2

--- a/solution.py
+++ b/solution.py
@@ -30,7 +30,7 @@
     groups, ranks,
     base, delta, mult, net, ang, ends, params, rating, status3, status, slack, zdual,
     mis_out, dual_out, lim_out, norm_out, tot_out,
-    bbuf, dbuf, mbuf, ebuf, pbuf, stbuf, table, got, vals, left, onehot, acc,
+    bbuf, dbuf, mbuf, ebuf, pbuf, stbuf, table, acc,
     res, rbuf, flow, rflow, sqs, sqbuf,
     send, recv, base_send, base_recv, sq_send, sq_recv,
 ):
@@ -98,7 +98,6 @@
     pbuf[me] = params[...]
     stbuf[me] = status3[me]
     table[...] = jnp.zeros_like(table)
-    vals[...] = jnp.zeros_like(vals)
     acc[...] = jnp.zeros_like(acc)
     sqs[...] = jnp.zeros_like(sqs)
     live_own = status[...].astype(jnp.float32)
@@ -122,11 +121,21 @@
     tiles = table.shape[1] // LANES
     high = table.shape[1] // SPAN
 
-    def one_source(src, carry):
-        def pick(t, c):
-            cols = pl.ds(pl.multiple_of(t * LANES, LANES), LANES)
-            for end in range(2):
-                spot = jnp.broadcast_to(ebuf[src, end : end + 1, cols], (ROWS, LANES))
+    chunk = SPAN if nl % SPAN == 0 else LANES
+    pieces = nl // chunk
+    bf16 = jnp.bfloat16
+
+    def place(i):
+        return i // pieces, pl.ds(pl.multiple_of(lax.rem(i, pieces) * chunk, chunk), chunk)
+
+    def pick(i):
+        src, cols = place(i)
+        picked = []
+        for end in range(2):
+            spots = jnp.broadcast_to(ebuf[src, end : end + 1, cols], (ROWS, chunk))
+            tiles_found = []
+            for at in range(0, chunk, LANES):
+                spot = spots[:, at : at + LANES]
                 low, tile = spot & (LANES - 1), spot >> 7
                 found = jnp.zeros((ROWS, LANES), jnp.float32)
                 for k in range(tiles):
@@ -134,19 +143,21 @@
                         table[:, k * LANES : (k + 1) * LANES], low, axis=1, mode="promise_in_bounds"
                     )
                     found = jnp.where(tile == k, piece, found)
-                got[end, :, cols] = found
-            return c
-
-        lax.fori_loop(0, nl // LANES, pick, 0)
+                tiles_found.append(found)
+            picked.append(jnp.concatenate(tiles_found, axis=1))
+        return tuple(picked)
+
+    def process(i, picked):
+        src, cols = place(i)
 
         def quantity(end, q):
-            return got[end, q * per : (q + 1) * per, :]
+            return picked[end][q * per : (q + 1) * per, :]
 
         vf, vt = quantity(0, 0), quantity(1, 0)
         sn, cs = sin_cos(quantity(0, 1) - quantity(1, 1))
-        par = pbuf[src]
+        par = pbuf[src, :, cols]
         g, b, h = par[0:1], par[1:2], par[2:3]
-        live = stbuf[src].astype(jnp.float32)
+        live = stbuf[src, :, cols].astype(jnp.float32)
         u = vf * vt
         gc_bs, gc_mbs = g * cs + b * sn, g * cs - b * sn
         gs_bc, gs_mbc = g * sn + b * cs, g * sn - b * cs
@@ -159,39 +170,34 @@
             quantity(0, 2) * gs_mbc - quantity(0, 3) * gc_bs
             + quantity(1, 2) * gs_bc + quantity(1, 3) * gc_mbs
         )
-        flow[src] = pf * pf + qf * qf
-        vals[0, 0:per, :] = pf
-        vals[0, per : 2 * per, :] = qf
-        vals[0, 2 * per : 3 * per, :] = fd
-        vals[1, 0:per, :] = pt
-        vals[1, per : 2 * per, :] = qt
-        vals[1, 2 * per : 3 * per, :] = -fd
-
-        for end in range(2):
-            def spread(t, c):
-                cols = pl.ds(pl.multiple_of(t * LANES, LANES), LANES)
-                spot = ebuf[src, end : end + 1, cols]
-                low = jnp.broadcast_to(spot & (SPAN - 1), (SPAN, LANES))
-                label = lax.broadcasted_iota(jnp.int32, (SPAN, LANES), 0)
-                onehot[:, cols] = jnp.where(low == label, 1.0, 0.0).astype(jnp.bfloat16)
-                row = jnp.broadcast_to(spot >> 8, (2 * ROWS, LANES))
-                value = vals[end, :, cols]
-                head = value.astype(jnp.bfloat16).astype(jnp.float32)
-                both = jnp.concatenate([head, value - head], axis=0)
-                for k in range(high):
-                    left[k * 2 * ROWS : (k + 1) * 2 * ROWS, cols] = jnp.where(
-                        row == k, both, 0.0
-                    ).astype(jnp.bfloat16)
-                return c
-
-            lax.fori_loop(0, nl // LANES, spread, 0)
-            acc[...] += lax.dot_general(
-                left[...], onehot[...], (((1,), (1,)), ((), ())),
-                preferred_element_type=jnp.float32,
-            )
-        return carry
-
-    lax.fori_loop(0, ranks, one_source, 0)
+        flow[src, :, cols] = pf * pf + qf * qf
+        blank = [jnp.zeros((ROWS - 3 * per, chunk), jnp.float32)]
+        lefts, hots = [], []
+        label = lax.broadcasted_iota(jnp.int32, (SPAN, chunk), 0).astype(bf16)
+        for end, terms in ((0, [pf, qf, fd]), (1, [pt, qt, -fd])):
+            value = jnp.concatenate(terms + blank, axis=0)
+            head = value.astype(bf16).astype(jnp.float32)
+            both = jnp.concatenate([head, value - head], axis=0).astype(bf16)
+            spot = ebuf[src, end : end + 1, cols]
+            row = jnp.broadcast_to(spot >> 8, (2 * ROWS, chunk)).astype(bf16)
+            low = jnp.broadcast_to((spot & (SPAN - 1)), (2 * ROWS, chunk)).astype(bf16)
+            low = jnp.concatenate([low] * (SPAN // (2 * ROWS)), axis=0)
+            hots.append(jnp.where(low == label, bf16(1), bf16(0)))
+            lefts.append(jnp.concatenate(
+                [jnp.where(row == bf16(k), both, bf16(0)) for k in range(high)], axis=0
+            ))
+        acc[...] += lax.dot_general(
+            jnp.concatenate(lefts, axis=1), jnp.concatenate(hots, axis=1),
+            (((1,), (1,)), ((), ())), preferred_element_type=jnp.float32,
+        )
+
+    def advance(i, picked):
+        following = pick(i)
+        process(i - 1, picked)
+        return following
+
+    last = lax.fori_loop(1, ranks * pieces, advance, pick(0))
+    process(ranks * pieces - 1, last)
 
     for k in range(high):
         at = k * SPAN
@@ -295,10 +301,6 @@
             pltpu.VMEM((ranks, 3, nl), f32),
             pltpu.VMEM((ranks, per, nl), jnp.int32),
             pltpu.VMEM((ROWS, buses), f32),
-            pltpu.VMEM((2, ROWS, nl), f32),
-            pltpu.VMEM((2, ROWS, nl), f32),
-            pltpu.VMEM((high * 2 * ROWS, nl), jnp.bfloat16),
-            pltpu.VMEM((SPAN, nl), jnp.bfloat16),
             pltpu.VMEM((high * 2 * ROWS, SPAN), f32),
             pltpu.VMEM((ranks, ROWS, nb), f32),
             pltpu.VMEM((ranks, ROWS, nb), f32),

time: 113 us -> 81 us (0.72)
  Pallas kernels: 102 us -> 70.6 us
    pallas_call x1, Pallas kernels: 102 us -> 70.6 us  [per_device(): pl.pallas_call(functools.partial(body, groups, ranks), out_shape=(jax.Sha...]
where the time goes in v3:
time: 81 us; the launch traced here: 80.6 us
  Pallas kernels  70.6 us (87%)
  local copies, waits for them, and re-layouts  9.08 us (11%)
  between operations  0.81 us (1%)
    pallas_call x1, Pallas kernels, per_device(): pl.pallas_call(functools.partial(body, groups, ranks), out_shape=(jax.Sha...  70.6 us
    unnamed x29, local copies, waits for them, and re-layouts  6.77 us

profile of v3, /device:TPU:0, one launch (start us, length us, event | category | flops | bytes accessed | tf_op | source)
XLA Modules:
  0.0 80.6 jit_solution(4176263927740645468)
XLA Ops:
  0.6 0.0 copy-start.11
  0.6 0.0 copy-start.10
  0.7 0.7 stack.30
  1.3 0.0 copy-done.11
  1.4 0.0 copy-start.7
  1.4 0.0 copy-start.8
  1.4 0.0 copy-start.9
  1.4 0.7 stack.33
  2.1 0.0 copy-done.7
  2.1 0.0 copy-start.2
  2.2 0.0 copy-done.8
  2.2 0.0 copy-start
  2.3 0.0 copy-done.9
  2.3 0.0 copy-done.10
  2.3 0.0 copy-start.1
  2.4 0.8 broadcast_in_dim.3.rating
  3.1 0.0 copy-done
  3.2 0.1 reshape.13.status3
  3.2 0.0 copy-done.2
  3.2 0.0 copy-done.1
  3.3 0.9 %copy-done.3 = f32[8,2,2560]{2,1,0:T(2,128)S(1)} copy-done((f32[8,2,2560]{2,1,0:T(2,128)S(1)}, f32[8,2,2560]{2,1,0:T(2,128)}, u32[]{:S(2)}) %copy-start.3) | copy-done | bytes 163864
  4.2 0.0 copy-start.4
  4.2 0.9 %copy-done.4 = f32[8,3328]{1,0:T(8,128)S(1)} copy-done((f32[8,3328]{1,0:T(8,128)S(1)}, f32[8,3328]{1,0:T(8,128)}, u32[]{:S(2)}) %copy-start.4) | copy-done | bytes 106520
  5.1 0.0 copy-start.5
  5.1 0.9 %copy-done.5 = f32[8,3328]{1,0:T(8,128)S(1)} copy-done((f32[8,3328]{1,0:T(8,128)S(1)}, f32[8,3328]{1,0:T(8,128)}, u32[]{:S(2)}) %copy-start.5) | copy-done | bytes 106520
  6.0 0.9 %copy-done.6 = f32[8,2560]{1,0:T(8,128)S(1)} copy-done((f32[8,2560]{1,0:T(8,128)S(1)}, f32[8,2560]{1,0:T(8,128)}, u32[]{:S(2)}) %copy-start.6) | copy-done | bytes 81944
  6.8 70.6 %shard_map.182 = (f32[8,2,2560]{2,1,0:T(2,128)S(1)}, f32[8,2560]{1,0:T(8,128)S(1)}, f32[8,3328]{1,0:T(8,128)S(1)}, f32[8,4]{1,0:T(8,128)S(1)}, f32[1,4]{1,0:T(1,128)S(1)}) custom-call(f32[2,320]{1,0:T(2,128)S(1)} %pad_maximum_fusion.1.base, f32[8,2,2560]{2,1,0:T(2,128)S(1)} %copy-done.1, f32[8,2,2560]{2,1,0:T(2,128)S(1)} %copy-done.2, ...), custom_call_target="tpu_custom_call" | custom-call | tf_op jit(solution)/shard_map/pallas_call | solution.py:285
  77.5 0.7 copy.20
  78.1 0.7 copy.25
  78.8 0.6 copy.26
  79.4 0.6 copy.27
  80.1 0.5 copy.28
  (10 shorter events, 0.1 us)
Async XLA Ops:
  0.6 0.7 copy-start.11
  0.6 1.6 %copy-start.10 = (f32[3328]{0:T(1024)S(1)}, f32[3328]{0:T(1024)}, u32[]{:S(2)}) copy-start(f32[3328]{0:T(1024)} %param.26) | copy-start | bytes 39940
  1.4 0.8 copy-start.7
  1.4 0.8 %copy-start.8 = (f32[3328]{0:T(1024)S(1)}, f32[3328]{0:T(1024)}, u32[]{:S(2)}) copy-start(f32[3328]{0:T(1024)} %param.24) | copy-start | bytes 39940
  1.4 0.9 %copy-start.9 = (f32[3328]{0:T(1024)S(1)}, f32[3328]{0:T(1024)}, u32[]{:S(2)}) copy-start(f32[3328]{0:T(1024)} %param.25) | copy-start | bytes 39940
  2.1 1.1 %copy-start.2 = (f32[8,2,2560]{2,1,0:T(2,128)S(1)}, f32[8,2,2560]{2,1,0:T(2,128)}, u32[]{:S(2)}) copy-start(f32[8,2,2560]{2,1,0:T(2,128)} %mult.1) | copy-start | bytes 491524
  2.2 0.9 %copy-start = (s32[8,3328]{1,0:T(8,128)S(1)}, s32[8,3328]{1,0:T(8,128)}, u32[]{:S(2)}) copy-start(s32[8,3328]{1,0:T(8,128)} %status.1) | copy-start | bytes 319492
  2.3 0.9 %copy-start.1 = (f32[8,2,2560]{2,1,0:T(2,128)S(1)}, f32[8,2,2560]{2,1,0:T(2,128)}, u32[]{:S(2)}) copy-start(f32[8,2,2560]{2,1,0:T(2,128)} %delta.1) | copy-start | bytes 491524
  3.3 0.9 %copy-start.3 = (f32[8,2,2560]{2,1,0:T(2,128)S(1)}, f32[8,2,2560]{2,1,0:T(2,128)}, u32[]{:S(2)}) copy-start(f32[8,2,2560]{2,1,0:T(2,128)} %net.1) | copy-start | bytes 491524
  4.2 0.9 %copy-start.4 = (f32[8,3328]{1,0:T(8,128)S(1)}, f32[8,3328]{1,0:T(8,128)}, u32[]{:S(2)}) copy-start(f32[8,3328]{1,0:T(8,128)} %slack.1) | copy-start | bytes 319492
  5.1 0.9 %copy-start.5 = (f32[8,3328]{1,0:T(8,128)S(1)}, f32[8,3328]{1,0:T(8,128)}, u32[]{:S(2)}) copy-start(f32[8,3328]{1,0:T(8,128)} %zdual.1) | copy-start | bytes 319492
  6.0 0.9 %copy-start.6 = (f32[8,2560]{1,0:T(8,128)S(1)}, f32[8,2560]{1,0:T(8,128)}, u32[]{:S(2)}) copy-start(f32[8,2560]{1,0:T(8,128)} %ang.1) | copy-start | bytes 245764

commit v4 on v3

--- a/solution.py
+++ b/solution.py
@@ -28,10 +28,11 @@
 
 def body(
     groups, ranks,
-    base, delta, mult, net, ang, ends, params, rating, status3, status, slack, zdual,
+    base, delta, mult, net_any, ang_any, ends, params, rating, status3, status_any, slack_any, zdual_any,
     mis_out, dual_out, lim_out, norm_out, tot_out,
     bbuf, dbuf, mbuf, ebuf, pbuf, stbuf, table, acc,
-    res, rbuf, flow, rflow, sqs, sqbuf,
+    res, rbuf, flow, rflow, sqs, sqbuf, rowbuf,
+    net, ang, status, slack, zdual, local,
     send, recv, base_send, base_recv, sq_send, sq_recv,
 ):
     grp, me = lax.axis_index("ctg"), lax.axis_index("br")
@@ -40,6 +41,18 @@
     per = dbuf.shape[1]
     nb, nl = delta.shape[2], ends.shape[1]
     scen = delta.shape[0]
+
+    own = pl.ds(me * per, per)
+    local_copies = [
+        pltpu.make_async_copy(a, b, local.at[i])
+        for i, (a, b) in enumerate((
+            (delta.at[own], dbuf.at[me]), (mult.at[own], mbuf.at[me]),
+            (status_any, status), (slack_any, slack), (zdual_any, zdual),
+            (net_any, net), (ang_any, ang),
+        ))
+    ]
+    for copy in local_copies:
+        copy.start()
 
     barrier = pltpu.get_barrier_semaphore()
 
@@ -90,23 +103,22 @@
         for group in first:
             group[kind].start()
 
-    own = pl.ds(me * per, per)
     bbuf[mine] = base[...]
-    dbuf[me] = delta[own]
-    mbuf[me] = mult[own]
     ebuf[me] = ends[...]
     pbuf[me] = params[...]
     stbuf[me] = status3[me]
     table[...] = jnp.zeros_like(table)
     acc[...] = jnp.zeros_like(acc)
     sqs[...] = jnp.zeros_like(sqs)
+    for copy in local_copies:
+        copy.wait()
     live_own = status[...].astype(jnp.float32)
     comp = live_own * (zdual[...] * slack[...] - 0.01)
     sqs[:, 3:4] = jnp.sum(comp * comp, axis=1, keepdims=True)
 
     lax.fori_loop(1, count, finish_base, 0)
     for group in first:
-        for copy in group:
+        for copy in group[:3]:
             copy.wait()
 
     for src in range(ranks):
@@ -126,7 +138,7 @@
     bf16 = jnp.bfloat16
 
     def place(i):
-        return i // pieces, pl.ds(pl.multiple_of(lax.rem(i, pieces) * chunk, chunk), chunk)
+        return lax.rem(me - i // pieces + ranks, ranks), pl.ds(pl.multiple_of(lax.rem(i, pieces) * chunk, chunk), chunk)
 
     def pick(i):
         src, cols = place(i)
@@ -191,78 +203,100 @@
             (((1,), (1,)), ((), ())), preferred_element_type=jnp.float32,
         )
 
-    def advance(i, picked):
-        following = pick(i)
-        process(i - 1, picked)
-        return following
-
-    last = lax.fori_loop(1, ranks * pieces, advance, pick(0))
-    process(ranks * pieces - 1, last)
+    final = ranks * pieces - 1
+
+    def one_step(step, picked):
+        src = lax.rem(me - step + ranks, ranks)
+
+        @pl.when(step > 0)
+        def _():
+            remote(params, pbuf.at[me], 3, step).wait()
+            remote(status3.at[0], stbuf.at[me], 4, step).wait()
+
+        def advance(t, picked):
+            i = step * pieces + t
+            following = pick(jnp.minimum(i + 1, final))
+            process(i, picked)
+            return following
+
+        picked = lax.fori_loop(0, pieces, advance, picked)
+
+        @pl.when(step > 0)
+        def _():
+            remote(flow.at[src], rflow.at[me], 6, ranks - step).start()
+
+        return picked
+
+    lax.fori_loop(0, ranks, one_step, pick(0))
 
     for k in range(high):
         at = k * SPAN
         row = k * 2 * ROWS
-        res[at // nb, :, at % nb : at % nb + SPAN] = (
-            acc[row : row + ROWS, :] + acc[row + ROWS : row + 2 * ROWS, :]
-        )
+        sums = acc[row : row + ROWS, :] + acc[row + ROWS : row + 2 * ROWS, :]
+        for q in range(3):
+            res[at // nb, q, :, at % nb : at % nb + SPAN] = sums[q * per : (q + 1) * per, :]
 
     back = []
     for step in range(1, ranks):
         peer = lax.rem(me + step, ranks)
         back.append((
             remote(res.at[peer], rbuf.at[me], 5, step),
-            remote(flow.at[peer], rflow.at[me], 6, step),
         ))
-    for kind in range(2):
-        for group in back:
-            group[kind].start()
+    for group in back:
+        group[0].start()
     rbuf[me] = res[me]
     rflow[me] = flow[me]
+    for step in range(1, ranks):
+        remote(flow.at[me], rflow.at[me], 6, step).wait()
     for group in back:
-        for copy in group:
-            copy.wait()
+        group[0].wait()
 
     rate = rating[...] * rating[...]
     for src in range(ranks):
-        sums = rbuf[src]
         for s in range(per):
             c = src * per + s
             total = jnp.zeros((1, 1), jnp.float32)
             for k in range(2):
-                row = sums[k * per + s : k * per + s + 1, :] - net[c, k : k + 1, :]
+                row = rbuf[src, k, s : s + 1, :] - net[c, k : k + 1, :]
                 mis_out[c, k : k + 1, :] = row
                 total = total + jnp.sum(row * row, axis=1, keepdims=True)
             sqs[c : c + 1, 0:1] = total
         rows = slice(src * per, (src + 1) * per)
-        dual = sums[2 * per : 3 * per, :] + ang[rows, :]
+        dual = rbuf[src, 2] + ang[rows, :]
         dual_out[rows, :] = dual
         sqs[rows, 1:2] = jnp.sum(dual * dual, axis=1, keepdims=True)
         lim = status[rows, :].astype(jnp.float32) * (rflow[src] + slack[rows, :] - rate)
         lim_out[rows, :] = lim
         sqs[rows, 2:3] = jnp.sum(lim * lim, axis=1, keepdims=True)
 
-    sqbuf[mine] = sqs[...]
+    sqbuf[me] = sqs[...]
+    rowbuf[mine] = jnp.sum(sqs[...], axis=0, keepdims=True)
+    near = [remote(sqbuf.at[me], sqbuf.at[me], 7, step) for step in range(1, ranks)]
+    for copy in near:
+        copy.start()
 
     def begin(i, c):
-        all_peers(sqbuf, sqbuf.at[mine], sq_send, sq_recv, i).start()
+        all_peers(rowbuf, rowbuf.at[mine], sq_send, sq_recv, i).start()
         return c
 
     def finish(i, c):
-        all_peers(sqbuf, sqbuf.at[mine], sq_send, sq_recv, i).wait()
+        all_peers(rowbuf, rowbuf.at[mine], sq_send, sq_recv, i).wait()
         return c
 
     lax.fori_loop(1, count, begin, 0)
+    for copy in near:
+        copy.wait()
     lax.fori_loop(1, count, finish, 0)
 
     def add(i, c):
-        return c + sqbuf[i]
+        return c + rowbuf[i]
 
     zero = jnp.zeros((scen, LANES), jnp.float32)
     group_sum = zero
     for z in range(ranks):
-        group_sum = group_sum + sqbuf[grp * ranks + z]
+        group_sum = group_sum + sqbuf[z]
     norm_out[...] = jnp.sqrt(group_sum[:, 0:4])
-    everything = jnp.sum(lax.fori_loop(0, count, add, zero), axis=0, keepdims=True)
+    everything = lax.fori_loop(0, count, add, jnp.zeros((1, LANES), jnp.float32))
     tot_out[...] = jnp.sqrt(everything[:, 0:4] / (scen * groups))
 
 
@@ -282,6 +316,7 @@
     params = jnp.stack([conduct, suscept, charging])
     f32 = jnp.float32
     vmem = pl.BlockSpec(memory_space=pltpu.VMEM)
+    hbm = pl.BlockSpec(memory_space=pl.ANY)
     mis, dual, lim, norms, tot = pl.pallas_call(
         functools.partial(body, groups, ranks),
         out_shape=(
@@ -291,7 +326,7 @@
             jax.ShapeDtypeStruct((scen, 4), f32),
             jax.ShapeDtypeStruct((1, 4), f32),
         ),
-        in_specs=[vmem] * 12,
+        in_specs=[vmem, hbm, hbm, hbm, hbm, vmem, vmem, vmem, vmem, hbm, hbm, hbm],
         out_specs=(vmem,) * 5,
         scratch_shapes=[
             pltpu.VMEM((count, 2, base_vm.shape[0]), f32),
@@ -302,14 +337,21 @@
             pltpu.VMEM((ranks, per, nl), jnp.int32),
             pltpu.VMEM((ROWS, buses), f32),
             pltpu.VMEM((high * 2 * ROWS, SPAN), f32),
-            pltpu.VMEM((ranks, ROWS, nb), f32),
-            pltpu.VMEM((ranks, ROWS, nb), f32),
+            pltpu.VMEM((ranks, 3, per, nb), f32),
+            pltpu.VMEM((ranks, 3, per, nb), f32),
             pltpu.VMEM((ranks, per, nl), f32),
             pltpu.VMEM((ranks, per, nl), f32),
             pltpu.VMEM((scen, LANES), f32),
-            pltpu.VMEM((count, scen, LANES), f32),
-            pltpu.SemaphoreType.DMA((7, ranks)),
-            pltpu.SemaphoreType.DMA((7, ranks)),
+            pltpu.VMEM((ranks, scen, LANES), f32),
+            pltpu.VMEM((count, 1, LANES), f32),
+            pltpu.VMEM((scen, 2, nb), f32),
+            pltpu.VMEM((scen, nb), f32),
+            pltpu.VMEM((scen, nl), jnp.int32),
+            pltpu.VMEM((scen, nl), f32),
+            pltpu.VMEM((scen, nl), f32),
+            pltpu.SemaphoreType.DMA((7,)),
+            pltpu.SemaphoreType.DMA((8, ranks)),
+            pltpu.SemaphoreType.DMA((8, ranks)),
             pltpu.SemaphoreType.DMA((count,)),
             pltpu.SemaphoreType.DMA((count,)),
             pltpu.SemaphoreType.DMA((count,)),

time: 81 us -> 74.3 us (0.917)
  Pallas kernels: 70.6 us -> 64 us
    pallas_call x1, Pallas kernels: 70.6 us -> 64 us  [per_device(): pl.pallas_call(functools.partial(body, groups, ranks), out_shape=(jax.Sha...]
where the time goes in v4:
time: 74.3 us; the launch traced here: 73.9 us
  Pallas kernels  64 us (86%)
  local copies, waits for them, and re-layouts  9.08 us (12%)
  between operations  0.81 us (1%)
    pallas_call x1, Pallas kernels, per_device(): pl.pallas_call(functools.partial(body, groups, ranks), out_shape=(jax.Sha...  64 us
    unnamed x29, local copies, waits for them, and re-layouts  6.77 us

profile of v4, /device:TPU:0, one launch (start us, length us, event | category | flops | bytes accessed | tf_op | source)
XLA Modules:
  0.0 73.9 jit_solution(6968746084996776235)
XLA Ops:
  0.6 0.0 copy-start.11
  0.6 0.0 copy-start.10
  0.7 0.7 stack.30
  1.3 0.0 copy-done.11
  1.4 0.0 copy-start.7
  1.4 0.0 copy-start.8
  1.4 0.0 copy-start.9
  1.4 0.7 stack.33
  2.1 0.0 copy-done.7
  2.1 0.0 copy-start.2
  2.2 0.0 copy-done.8
  2.2 0.0 copy-start
  2.3 0.0 copy-done.9
  2.3 0.0 copy-done.10
  2.3 0.0 copy-start.1
  2.4 0.8 %broadcast_in_dim.3.rating = f32[1,3328]{1,0:T(1,128)S(1)} reshape(f32[3328]{0:T(1024)} %param.27) | data formatting | bytes 26624 | tf_op jit(solution)/shard_map/broadcast_in_dim | solution.py:364
  3.1 0.0 copy-done
  3.2 0.1 reshape.13.status3
  3.2 0.0 copy-done.2
  3.2 0.0 copy-done.1
  3.3 0.0 copy-start.3
  3.3 0.9 %copy-done.3 = f32[8,2,2560]{2,1,0:T(2,128)S(1)} copy-done((f32[8,2,2560]{2,1,0:T(2,128)S(1)}, f32[8,2,2560]{2,1,0:T(2,128)}, u32[]{:S(2)}) %copy-start.3) | copy-done | bytes 163864
  4.2 0.0 copy-start.4
  4.2 0.9 %copy-done.4 = f32[8,3328]{1,0:T(8,128)S(1)} copy-done((f32[8,3328]{1,0:T(8,128)S(1)}, f32[8,3328]{1,0:T(8,128)}, u32[]{:S(2)}) %copy-start.4) | copy-done | bytes 106520
  5.1 0.9 %copy-done.5 = f32[8,3328]{1,0:T(8,128)S(1)} copy-done((f32[8,3328]{1,0:T(8,128)S(1)}, f32[8,3328]{1,0:T(8,128)}, u32[]{:S(2)}) %copy-start.5) | copy-done | bytes 106520
  6.0 0.9 %copy-done.6 = f32[8,2560]{1,0:T(8,128)S(1)} copy-done((f32[8,2560]{1,0:T(8,128)S(1)}, f32[8,2560]{1,0:T(8,128)}, u32[]{:S(2)}) %copy-start.6) | copy-done | bytes 81944
  6.8 64.0 %shard_map.182 = (f32[8,2,2560]{2,1,0:T(2,128)S(1)}, f32[8,2560]{1,0:T(8,128)S(1)}, f32[8,3328]{1,0:T(8,128)S(1)}, f32[8,4]{1,0:T(8,128)S(1)}, f32[1,4]{1,0:T(1,128)S(1)}) custom-call(f32[2,320]{1,0:T(2,128)S(1)} %pad_maximum_fusion.1.base, f32[8,2,2560]{2,1,0:T(2,128)S(1)} %copy-done.1, f32[8,2,2560]{2,1,0:T(2,128)S(1)} %copy-done.2, ...), custom_call_target="tpu_custom_call" | custom-call | tf_op jit(solution)/shard_map/pallas_call | solution.py:320
  70.8 0.7 copy.20
  71.5 0.7 copy.25
  72.1 0.6 copy.26
  72.8 0.6 copy.27
  73.4 0.5 copy.28
  (10 shorter events, 0.1 us)
Async XLA Ops:
  0.6 0.7 copy-start.11
  0.6 1.6 %copy-start.10 = (f32[3328]{0:T(1024)S(1)}, f32[3328]{0:T(1024)}, u32[]{:S(2)}) copy-start(f32[3328]{0:T(1024)} %param.26) | copy-start | bytes 39940
  1.4 0.8 %copy-start.7 = (s32[3328]{0:T(1024)S(1)}, s32[3328]{0:T(1024)}, u32[]{:S(2)}) copy-start(s32[3328]{0:T(1024)} %param.22) | copy-start | bytes 39940
  1.4 0.8 %copy-start.8 = (f32[3328]{0:T(1024)S(1)}, f32[3328]{0:T(1024)}, u32[]{:S(2)}) copy-start(f32[3328]{0:T(1024)} %param.24) | copy-start | bytes 39940
  1.4 0.9 %copy-start.9 = (f32[3328]{0:T(1024)S(1)}, f32[3328]{0:T(1024)}, u32[]{:S(2)}) copy-start(f32[3328]{0:T(1024)} %param.25) | copy-start | bytes 39940
  2.1 1.1 %copy-start.2 = (f32[8,2,2560]{2,1,0:T(2,128)S(1)}, f32[8,2,2560]{2,1,0:T(2,128)}, u32[]{:S(2)}) copy-start(f32[8,2,2560]{2,1,0:T(2,128)} %mult.1) | copy-start | bytes 491524
  2.2 0.9 %copy-start = (s32[8,3328]{1,0:T(8,128)S(1)}, s32[8,3328]{1,0:T(8,128)}, u32[]{:S(2)}) copy-start(s32[8,3328]{1,0:T(8,128)} %status_any.1) | copy-start | bytes 319492
  2.3 0.9 %copy-start.1 = (f32[8,2,2560]{2,1,0:T(2,128)S(1)}, f32[8,2,2560]{2,1,0:T(2,128)}, u32[]{:S(2)}) copy-start(f32[8,2,2560]{2,1,0:T(2,128)} %delta.1) | copy-start | bytes 491524
  3.3 0.9 %copy-start.3 = (f32[8,2,2560]{2,1,0:T(2,128)S(1)}, f32[8,2,2560]{2,1,0:T(2,128)}, u32[]{:S(2)}) copy-start(f32[8,2,2560]{2,1,0:T(2,128)} %net_any.1) | copy-start | bytes 491524
  4.2 0.9 %copy-start.4 = (f32[8,3328]{1,0:T(8,128)S(1)}, f32[8,3328]{1,0:T(8,128)}, u32[]{:S(2)}) copy-start(f32[8,3328]{1,0:T(8,128)} %slack_any.1) | copy-start | bytes 319492
  5.1 0.9 %copy-start.5 = (f32[8,3328]{1,0:T(8,128)S(1)}, f32[8,3328]{1,0:T(8,128)}, u32[]{:S(2)}) copy-start(f32[8,3328]{1,0:T(8,128)} %zdual_any.1) | copy-start | bytes 319492
  6.0 0.9 %copy-start.6 = (f32[8,2560]{1,0:T(8,128)S(1)}, f32[8,2560]{1,0:T(8,128)}, u32[]{:S(2)}) copy-start(f32[8,2560]{1,0:T(8,128)} %ang_any.1) | copy-start | bytes 245764

commit v5 on v4

--- a/solution.py
+++ b/solution.py
@@ -270,33 +270,40 @@
         sqs[rows, 2:3] = jnp.sum(lim * lim, axis=1, keepdims=True)
 
     sqbuf[me] = sqs[...]
-    rowbuf[mine] = jnp.sum(sqs[...], axis=0, keepdims=True)
     near = [remote(sqbuf.at[me], sqbuf.at[me], 7, step) for step in range(1, ranks)]
     for copy in near:
         copy.start()
-
-    def begin(i, c):
-        all_peers(rowbuf, rowbuf.at[mine], sq_send, sq_recv, i).start()
-        return c
-
-    def finish(i, c):
-        all_peers(rowbuf, rowbuf.at[mine], sq_send, sq_recv, i).wait()
-        return c
-
-    lax.fori_loop(1, count, begin, 0)
     for copy in near:
         copy.wait()
-    lax.fori_loop(1, count, finish, 0)
-
-    def add(i, c):
-        return c + rowbuf[i]
-
-    zero = jnp.zeros((scen, LANES), jnp.float32)
-    group_sum = zero
+    group_sum = jnp.zeros((scen, LANES), jnp.float32)
     for z in range(ranks):
         group_sum = group_sum + sqbuf[z]
     norm_out[...] = jnp.sqrt(group_sum[:, 0:4])
-    everything = lax.fori_loop(0, count, add, jnp.zeros((1, LANES), jnp.float32))
+
+    rowbuf[grp] = jnp.sum(group_sum, axis=0, keepdims=True)
+
+    def across(i):
+        return pltpu.make_async_remote_copy(
+            src_ref=rowbuf.at[grp], dst_ref=rowbuf.at[grp],
+            send_sem=sq_send.at[i], recv_sem=sq_recv.at[i],
+            device_id=(lax.rem(grp + i, groups), me), device_id_type=MESH,
+        )
+
+    def begin(i, c):
+        across(i).start()
+        return c
+
+    def finish(i, c):
+        across(i).wait()
+        return c
+
+    lax.fori_loop(1, groups, begin, 0)
+    lax.fori_loop(1, groups, finish, 0)
+
+    def add(i, c):
+        return c + rowbuf[i]
+
+    everything = lax.fori_loop(0, groups, add, jnp.zeros((1, LANES), jnp.float32))
     tot_out[...] = jnp.sqrt(everything[:, 0:4] / (scen * groups))
 
 
@@ -343,7 +350,7 @@
             pltpu.VMEM((ranks, per, nl), f32),
             pltpu.VMEM((scen, LANES), f32),
             pltpu.VMEM((ranks, scen, LANES), f32),
-            pltpu.VMEM((count, 1, LANES), f32),
+            pltpu.VMEM((groups, 1, LANES), f32),
             pltpu.VMEM((scen, 2, nb), f32),
             pltpu.VMEM((scen, nb), f32),
             pltpu.VMEM((scen, nl), jnp.int32),

time: 74.3 us -> 75.8 us (1.020)
  Pallas kernels: 64 us -> 65.4 us
    pallas_call x1, Pallas kernels: 64 us -> 65.4 us  [per_device(): pl.pallas_call(functools.partial(body, groups, ranks), out_shape=(jax.Sha...]
where the time goes in v5:
time: 75.8 us; the launch traced here: 75.4 us
  Pallas kernels  65.4 us (86%)
  local copies, waits for them, and re-layouts  9.08 us (12%)
  between operations  0.81 us (1%)
    pallas_call x1, Pallas kernels, per_device(): pl.pallas_call(functools.partial(body, groups, ranks), out_shape=(jax.Sha...  65.4 us
    unnamed x29, local copies, waits for them, and re-layouts  6.77 us

profile of v5, /device:TPU:0, one launch (start us, length us, event | category | flops | bytes accessed | tf_op | source)
XLA Modules:
  0.0 75.4 jit_solution(12148040072180673634)
XLA Ops:
  0.6 0.0 copy-start.11
  0.6 0.0 copy-start.10
  0.7 0.7 stack.30
  1.3 0.0 copy-done.11
  1.4 0.0 copy-start.8
  1.4 0.0 copy-start.9
  1.4 0.7 stack.33
  2.1 0.0 copy-done.7
  2.1 0.0 copy-start.2
  2.2 0.0 copy-done.8
  2.2 0.0 copy-start
  2.3 0.0 copy-done.9
  2.3 0.0 copy-done.10
  2.3 0.0 copy-start.1
  2.4 0.8 %broadcast_in_dim.3.rating = f32[1,3328]{1,0:T(1,128)S(1)} reshape(f32[3328]{0:T(1024)} %param.27) | data formatting | bytes 26624 | tf_op jit(solution)/shard_map/broadcast_in_dim | solution.py:371
  3.1 0.0 copy-done
  3.2 0.1 reshape.13.status3
  3.2 0.0 copy-done.2
  3.2 0.0 copy-done.1
  3.3 0.0 copy-start.3
  3.3 0.9 %copy-done.3 = f32[8,2,2560]{2,1,0:T(2,128)S(1)} copy-done((f32[8,2,2560]{2,1,0:T(2,128)S(1)}, f32[8,2,2560]{2,1,0:T(2,128)}, u32[]{:S(2)}) %copy-start.3) | copy-done | bytes 163864
  4.2 0.0 copy-start.4
  4.2 0.9 %copy-done.4 = f32[8,3328]{1,0:T(8,128)S(1)} copy-done((f32[8,3328]{1,0:T(8,128)S(1)}, f32[8,3328]{1,0:T(8,128)}, u32[]{:S(2)}) %copy-start.4) | copy-done | bytes 106520
  5.1 0.0 copy-start.5
  5.1 0.9 %copy-done.5 = f32[8,3328]{1,0:T(8,128)S(1)} copy-done((f32[8,3328]{1,0:T(8,128)S(1)}, f32[8,3328]{1,0:T(8,128)}, u32[]{:S(2)}) %copy-start.5) | copy-done | bytes 106520
  6.0 0.9 %copy-done.6 = f32[8,2560]{1,0:T(8,128)S(1)} copy-done((f32[8,2560]{1,0:T(8,128)S(1)}, f32[8,2560]{1,0:T(8,128)}, u32[]{:S(2)}) %copy-start.6) | copy-done | bytes 81944
  6.8 65.4 %shard_map.182 = (f32[8,2,2560]{2,1,0:T(2,128)S(1)}, f32[8,2560]{1,0:T(8,128)S(1)}, f32[8,3328]{1,0:T(8,128)S(1)}, f32[8,4]{1,0:T(8,128)S(1)}, f32[1,4]{1,0:T(1,128)S(1)}) custom-call(f32[2,320]{1,0:T(2,128)S(1)} %pad_maximum_fusion.1.base, f32[8,2,2560]{2,1,0:T(2,128)S(1)} %copy-done.1, f32[8,2,2560]{2,1,0:T(2,128)S(1)} %copy-done.2, ...), custom_call_target="tpu_custom_call" | custom-call | tf_op jit(solution)/shard_map/pallas_call | solution.py:327
  72.3 0.7 copy.20
  72.9 0.7 copy.25
  73.6 0.6 copy.26
  74.2 0.6 copy.27
  74.9 0.5 copy.28
  (10 shorter events, 0.1 us)
Async XLA Ops:
  0.6 0.7 copy-start.11
  0.6 1.6 %copy-start.10 = (f32[3328]{0:T(1024)S(1)}, f32[3328]{0:T(1024)}, u32[]{:S(2)}) copy-start(f32[3328]{0:T(1024)} %param.26) | copy-start | bytes 39940
  1.4 0.8 %copy-start.7 = (s32[3328]{0:T(1024)S(1)}, s32[3328]{0:T(1024)}, u32[]{:S(2)}) copy-start(s32[3328]{0:T(1024)} %param.22) | copy-start | bytes 39940
  1.4 0.8 %copy-start.8 = (f32[3328]{0:T(1024)S(1)}, f32[3328]{0:T(1024)}, u32[]{:S(2)}) copy-start(f32[3328]{0:T(1024)} %param.24) | copy-start | bytes 39940
  1.4 0.9 %copy-start.9 = (f32[3328]{0:T(1024)S(1)}, f32[3328]{0:T(1024)}, u32[]{:S(2)}) copy-start(f32[3328]{0:T(1024)} %param.25) | copy-start | bytes 39940
  2.1 1.1 %copy-start.2 = (f32[8,2,2560]{2,1,0:T(2,128)S(1)}, f32[8,2,2560]{2,1,0:T(2,128)}, u32[]{:S(2)}) copy-start(f32[8,2,2560]{2,1,0:T(2,128)} %mult.1) | copy-start | bytes 491524
  2.2 0.9 %copy-start = (s32[8,3328]{1,0:T(8,128)S(1)}, s32[8,3328]{1,0:T(8,128)}, u32[]{:S(2)}) copy-start(s32[8,3328]{1,0:T(8,128)} %status_any.1) | copy-start | bytes 319492
  2.3 0.9 %copy-start.1 = (f32[8,2,2560]{2,1,0:T(2,128)S(1)}, f32[8,2,2560]{2,1,0:T(2,128)}, u32[]{:S(2)}) copy-start(f32[8,2,2560]{2,1,0:T(2,128)} %delta.1) | copy-start | bytes 491524
  3.3 0.9 %copy-start.3 = (f32[8,2,2560]{2,1,0:T(2,128)S(1)}, f32[8,2,2560]{2,1,0:T(2,128)}, u32[]{:S(2)}) copy-start(f32[8,2,2560]{2,1,0:T(2,128)} %net_any.1) | copy-start | bytes 491524
  4.2 0.9 %copy-start.4 = (f32[8,3328]{1,0:T(8,128)S(1)}, f32[8,3328]{1,0:T(8,128)}, u32[]{:S(2)}) copy-start(f32[8,3328]{1,0:T(8,128)} %slack_any.1) | copy-start | bytes 319492
  5.1 0.9 %copy-start.5 = (f32[8,3328]{1,0:T(8,128)S(1)}, f32[8,3328]{1,0:T(8,128)}, u32[]{:S(2)}) copy-start(f32[8,3328]{1,0:T(8,128)} %zdual_any.1) | copy-start | bytes 319492
  6.0 0.9 %copy-start.6 = (f32[8,2560]{1,0:T(8,128)S(1)}, f32[8,2560]{1,0:T(8,128)}, u32[]{:S(2)}) copy-start(f32[8,2560]{1,0:T(8,128)} %ang_any.1) | copy-start | bytes 245764
